TPU v7x, 128 devices: a whole 4x4x4 slice. The times are simulated.
128 devices in a mesh: dp: 32 (over y, z, core), rep: 4 (over x).
Axes of the slice: x: 4, y: 4, z: 4, core: 2. Of those that a mesh axis runs over, the one named last changes fastest.
Arguments:
- enc: bfloat16 [256, 48, 640], P(('dp', 'rep')), may hold values from -6 to 6
- pred: bfloat16 [256, 17, 640], P(('dp', 'rep')), may hold values from -6 to 6
- labels: int32 [256, 16], P(('dp', 'rep')), may hold values from 1 to 4095
- frame_len: int32 [256], P(('dp', 'rep')), may hold values from 24 to 48, as said below
- label_len: int32 [256], P(('dp', 'rep')), may hold values from 1 to 16, as said below
- w_enc: bfloat16 [640, 640], replicated, may hold values from -0.25 to 0.25
- w_pred: bfloat16 [640, 640], replicated, may hold values from -0.25 to 0.25
- b_joint: bfloat16 [640], replicated, may hold values from -3 to 3
- w_out: bfloat16 [640, 4096], replicated, may hold values from -0.69921875 to 0.69921875
- b_out: bfloat16 [4096], replicated, may hold values from -5 to 5
Outputs:
- step_enc: float32 [640, 640], replicated
- step_pred: float32 [640, 640], replicated
- step_out: float32 [640, 4096], replicated
- step_bias_out: float32 [4096], replicated
- step_bias_joint: float32 [640], replicated
- mean_loss: float32 [], replicated
Inputs may be any that keep to these rules, and one draw needn't show every extreme that they name: `frame_len`: the last utterance has all 48 frames. `label_len`: the last utterance has all 16 labels.
All inputs are finite; a program needn't handle non-finite values.
Results may differ from a plain program's by a relative error of at most 0.0055.
Values sent between devices are 32-bit elements; how exact they have to be, the bound alone decides.
A program may use at most 256 MiB of HBM per device.

v0:
```python
import jax
import jax.numpy as jnp
from jax import lax
from jax.sharding import Mesh
from jax.sharding import PartitionSpec as P

DP_REP = ("dp_0", "dp_1", "dp_2", "rep")


NEG = -1e30
EPS = 1e-06


def by_axis(value, axes):
    for axis in axes:
        value = lax.psum(value, axis)
    return value


def diagonal_index(num_frames, count_labels):
    diagonals = jnp.arange(num_frames + count_labels - 1, dtype=jnp.int32)
    positions = jnp.arange(count_labels, dtype=jnp.int32)
    return diagonals[:, None] - positions[None, :]


def skewed(grid):
    utterances, num_frames, count_labels = grid.shape
    positions = jnp.arange(count_labels, dtype=jnp.int32)
    frame_index = diagonal_index(num_frames, count_labels)
    inside = (frame_index >= 0) & (frame_index < num_frames)
    picked = grid[:, jnp.clip(frame_index, 0, num_frames - 1), positions[None, :]]
    picked = jnp.where(inside[None, :, :], picked, NEG)
    return jnp.transpose(picked, (1, 0, 2))


def unskewed(diag_grid, num_frames):
    count_labels = diag_grid.shape[2]
    by_utterance = jnp.transpose(diag_grid, (1, 0, 2))
    frame_ids = jnp.arange(num_frames, dtype=jnp.int32)
    positions = jnp.arange(count_labels, dtype=jnp.int32)
    return by_utterance[:, frame_ids[:, None] + positions[None, :], positions[None, :]]


def lattice(blank, emit, frame_len, label_len):
    utterances, num_frames, count_labels = blank.shape
    positions = jnp.arange(count_labels, dtype=jnp.int32)
    frame_index = diagonal_index(num_frames, count_labels)
    blank_diag = skewed(blank)
    emit_diag = skewed(emit)
    neg_block = jnp.full((1, utterances, count_labels), NEG, jnp.float32)
    neg_col = jnp.full((utterances, 1), NEG, jnp.float32)
    neg_grid = jnp.full((utterances, count_labels), NEG, jnp.float32)
    frame_count = frame_len[:, None]
    label_count = label_len[:, None]
    terminal = jnp.where(positions[None, :] == label_count, 0.0, NEG).astype(jnp.float32)
    first_diag = jnp.broadcast_to(
        jnp.where(positions == 0, 0.0, NEG).astype(jnp.float32)[None, :], (utterances, count_labels)
    )
    blank_prev = jnp.concatenate([neg_block, blank_diag[:-1]], axis=0)
    emit_prev = jnp.concatenate([neg_block, emit_diag[:-1]], axis=0)
    steps_total = frame_index.shape[0]
    step_ids = jnp.arange(steps_total, dtype=jnp.int32)

    def both_ways(carry, inputs):
        alpha_prev, beta_next = carry
        step_id, blank_fwd, emit_fwd, frames_fwd, blank_back, emit_back, frames_back = inputs
        top_term = alpha_prev + blank_fwd
        left_term = jnp.concatenate([neg_col, (alpha_prev + emit_fwd)[:, :-1]], axis=1)
        alpha_cell = jnp.logaddexp(top_term, left_term)
        inside = (frames_fwd >= 0) & (frames_fwd < num_frames)
        alpha_cell = jnp.where(inside[None, :], alpha_cell, NEG)
        alpha_cell = jnp.where(step_id == 0, first_diag, alpha_cell)
        frames_row = frames_back[None, :]
        below = jnp.where(
            frames_row == frame_count - 1,
            terminal,
            jnp.where(frames_row >= frame_count, neg_grid, beta_next),
        )
        right_term = jnp.concatenate([beta_next[:, 1:], neg_col], axis=1)
        beta_cell = jnp.logaddexp(below + blank_back, right_term + emit_back)
        live = (positions[None, :] <= label_count) & (frames_row < frame_count) & (frames_row >= 0)
        beta_cell = jnp.where(live, beta_cell, NEG)
        return ((alpha_cell, beta_cell), (alpha_cell, beta_cell, below))

    inputs = (
        step_ids,
        blank_prev,
        emit_prev,
        frame_index,
        jnp.flip(blank_diag, 0),
        jnp.flip(emit_diag, 0),
        jnp.flip(frame_index, 0),
    )
    unused_last, (alpha_diag, beta_rev, below_rev) = lax.scan(
        both_ways, (first_diag, neg_grid), inputs
    )
    alpha = unskewed(alpha_diag, num_frames)
    beta = unskewed(jnp.flip(beta_rev, 0), num_frames)
    below = unskewed(jnp.flip(below_rev, 0), num_frames)
    return (alpha, beta, below)


def joint_forward(enc_row, pred_row, label_row, w_enc, w_pred, b_joint, w_out, b_out):
    num_frames = enc_row.shape[0]
    count_labels = pred_row.shape[0]
    joint_width = w_enc.shape[1]
    vocab_size = w_out.shape[1]
    enc_proj = jnp.dot(enc_row, w_enc, preferred_element_type=jnp.float32)
    pred_proj = jnp.dot(pred_row, w_pred, preferred_element_type=jnp.float32) + b_joint.astype(
        jnp.float32
    )
    hidden = jnp.tanh(enc_proj[:, None, :] + pred_proj[None, :, :]).astype(jnp.bfloat16)
    hidden = lax.optimization_barrier(hidden.reshape(num_frames * count_labels, joint_width))
    logits = jnp.dot(hidden, w_out, preferred_element_type=jnp.float32) + b_out.astype(jnp.float32)
    log_probs = jax.nn.log_softmax(logits, axis=-1)
    targets = jnp.concatenate([label_row, jnp.ones((1,), jnp.int32)])
    target_cols = jnp.tile(targets, num_frames)
    vocab_pos = jnp.arange(vocab_size, dtype=jnp.int32)
    is_target = vocab_pos[None, :] == target_cols[:, None]
    emit = jnp.sum(jnp.where(is_target, log_probs, 0.0), axis=1).reshape(num_frames, count_labels)
    blank = log_probs[:, 0].reshape(num_frames, count_labels)
    return (hidden, log_probs, blank, emit)


def joint_backward(
    enc_row, pred_row, label_row, hidden, log_probs, blank, emit, alpha, beta, below, w_out
):
    num_frames = enc_row.shape[0]
    count_labels = pred_row.shape[0]
    joint_width = hidden.shape[1]
    vocab_size = w_out.shape[1]
    targets = jnp.concatenate([label_row, jnp.ones((1,), jnp.int32)])
    target_cols = jnp.tile(targets, num_frames)
    vocab_pos = jnp.arange(vocab_size, dtype=jnp.int32)
    is_target = vocab_pos[None, :] == target_cols[:, None]
    log_total = beta[0, 0]
    right = jnp.concatenate([beta[:, 1:], jnp.full((num_frames, 1), NEG, jnp.float32)], axis=1)
    blank_occ = jnp.exp(alpha + blank + below - log_total).reshape(-1)
    emit_occ = jnp.exp(alpha + emit + right - log_total).reshape(-1)
    probs = jnp.exp(log_probs)
    grad_logits = probs * (blank_occ + emit_occ)[:, None]
    grad_logits = grad_logits - jnp.where(vocab_pos[None, :] == 0, blank_occ[:, None], 0.0)
    grad_logits = grad_logits - jnp.where(is_target, emit_occ[:, None], 0.0)
    grad_logits = lax.optimization_barrier(grad_logits.astype(jnp.bfloat16))
    grad_out = lax.dot_general(
        hidden, grad_logits, (((0,), (0,)), ((), ())), preferred_element_type=jnp.float32
    )
    grad_bias_out = jnp.sum(grad_logits.astype(jnp.float32), axis=0)
    grad_hidden = lax.dot_general(
        grad_logits, w_out, (((1,), (1,)), ((), ())), preferred_element_type=jnp.float32
    )
    hidden_wide = hidden.astype(jnp.float32)
    grad_pre = (grad_hidden * (1.0 - hidden_wide * hidden_wide)).reshape(
        num_frames, count_labels, joint_width
    )
    grad_enc_proj = lax.optimization_barrier(jnp.sum(grad_pre, axis=1).astype(jnp.bfloat16))
    grad_pred_proj = lax.optimization_barrier(jnp.sum(grad_pre, axis=0).astype(jnp.bfloat16))
    grad_enc = lax.dot_general(
        enc_row, grad_enc_proj, (((0,), (0,)), ((), ())), preferred_element_type=jnp.float32
    )
    grad_pred = lax.dot_general(
        pred_row, grad_pred_proj, (((0,), (0,)), ((), ())), preferred_element_type=jnp.float32
    )
    grad_bias_joint = jnp.sum(grad_pred_proj.astype(jnp.float32), axis=0)
    return (-log_total, (grad_enc, grad_pred, grad_out, grad_bias_out, grad_bias_joint))


def local_sums(enc, pred, labels, frame_len, label_len, w_enc, w_pred, b_joint, w_out, b_out):

    def forward_one(unused_carry, inputs):
        enc_row, pred_row, label_row = inputs
        return (
            None,
            joint_forward(enc_row, pred_row, label_row, w_enc, w_pred, b_joint, w_out, b_out),
        )

    unused_none, (hidden, log_probs, blank, emit) = lax.scan(forward_one, None, (enc, pred, labels))
    alpha, beta, below = lattice(blank, emit, frame_len, label_len)
    initial = (
        jnp.zeros(w_enc.shape, jnp.float32),
        jnp.zeros(w_pred.shape, jnp.float32),
        jnp.zeros(w_out.shape, jnp.float32),
        jnp.zeros(b_out.shape, jnp.float32),
        jnp.zeros(b_joint.shape, jnp.float32),
    )

    def backward_one(carry, inputs):
        loss_sum, grad_sums = carry
        loss_one, grads_one = joint_backward(*inputs, w_out)
        added = tuple((total + term for total, term in zip(grad_sums, grads_one)))
        return ((loss_sum + loss_one, added), None)

    (loss_sum, grads), unused_ys = lax.scan(
        backward_one,
        (jnp.float32(0.0), initial),
        (enc, pred, labels, hidden, log_probs, blank, emit, alpha, beta, below),
    )
    return (loss_sum, grads)


def squares(items):
    total_sq = jnp.float32(0.0)
    for item in items:
        total_sq = total_sq + jnp.sum(item * item)
    return total_sq


def per_device(enc, pred, labels, frame_len, label_len, w_enc, w_pred, b_joint, w_out, b_out):
    loss_local, grads = local_sums(
        enc, pred, labels, frame_len, label_len, w_enc, w_pred, b_joint, w_out, b_out
    )
    count_local = jnp.sum(label_len).astype(jnp.float32)
    param_count = jnp.float32(w_enc.size + w_pred.size + w_out.size + b_out.size + b_joint.size)
    loss_total, label_total = (by_axis(loss_local, DP_REP), by_axis(count_local, DP_REP))
    summed = lax.psum((grads[0], grads[1], grads[2], grads[3], grads[4]), DP_REP)
    scale = lax.rsqrt(squares(summed) / param_count + EPS)
    result = tuple((item * scale for item in summed))
    return (result[0], result[1], result[2], result[3], result[4], loss_total / label_total)


def solution(mesh):
    split = Mesh(mesh.devices.reshape(4, 4, 2, mesh.shape["rep"]), ("dp_0", "dp_1", "dp_2", "rep"))
    in_specs = (
        P(DP_REP, None, None),
        P(DP_REP, None, None),
        P(DP_REP, None),
        P(DP_REP),
        P(DP_REP),
        P(),
        P(),
        P(),
        P(),
        P(),
    )
    out_specs = (P(), P(), P(), P(), P(), P())
    return jax.shard_map(
        per_device, mesh=split, in_specs=in_specs, out_specs=out_specs, check_vma=False
    )
```

profile of v0, /device:TPU:1, one launch (start us, length us, event | category | flops | bytes accessed | tf_op | source)
XLA Modules:
  0.0 574.8 jit_solution(5680427295816515835)
XLA Ops:
  11.1 88.6 %while.58 = (s32[]{:T(128)}, bf16[2,816,640]{2,1,0:T(8,128)(2,1)}, f32[2,816,4096]{2,1,0:T(8,128)}, f32[2,48,17]{2,1,0:T(8,128)S(1)}, f32[2,48,17]{2,1,0:T(8,128...) while((s32[]{:T(128)}, bf16[2,816,640]{2,1,0:T(8,128)(2,1)}, ...), condition=%wide.region_4.5_spmd, body=%wide.region_0.4_spmd.sunk | while | flops 4369261056 | bytes 147507888 | solution.py:177
  11.9 1.4 convolution_add_fusion.2
  13.3 1.5 fusion.76
  16.4 7.5 %add_reduce_fusion.2 = (f32[816]{0:T(1024)S(1)}, f32[816,4096]{1,0:T(8,128)S(1)}) fusion(f32[4096]{0:T(1024)S(1)} %convert_element_type.65, bf16[816,640]{1,0:T(8,128)(2,1)S(1)} %convert_element_type.64, bf16[640,4096]{1,0:T(8,128)(2,1)} %get-tuple-element.1149), kind=kOutput, calls=%fused_computation.66.clone.1 | convolution fusion | flops 4284873984 | bytes 19676352 | tf_op jit(solution)/shard_map/while/body/eval_jaxpr/dot_general | solution.py:114
  23.9 2.3 exponential_reduce_fusion.2
  26.2 2.5 copy-done.1
  28.9 12.7 %select_reduce_fusion.2 = (f32[816]{0:T(1024)S(1)}, f32[816,4096]{1,0:T(8,128)}) fusion(s32[816]{0:T(1024)S(1)} %eq.178, f32[816]{0:T(1024)S(1)} %log.11, f32[816]{0:T(1024)S(1)} %get-tuple-element.1059, f32[816,4096]{1,0:T(8,128)} %copy-done.1, f32[4096]{0:T(1024)S(1)} %convert_element_type.65), kind=kLoop, calls=%fused_computation.62.clone.1 | loop fusion | flops 20053200 | bytes 26768128 | tf_op jit(solution)/shard_map/while/body/eval_jaxpr/reduce_sum | solution.py:120
  41.6 1.2 slice_reduce_fusion.2
  43.1 11.3 %bitcast_dynamic-update-slice_fusion.5 = f32[2,816,4096]{2,1,0:T(8,128)} fusion(f32[2,816,4096]{2,1,0:T(8,128)} %get-tuple-element.1126, s32[]{:T(128)} %get-tuple-element.1124, f32[816,4096]{1,0:T(8,128)} %get-tuple-element.1060), kind=kLoop, calls=%fused_computation.61.clone.1 | loop fusion | bytes 26739200 | tf_op jit(solution)/shard_map/while/body/jit(dynamic_update_index_in_dim)/dynamic_update_slice | solution.py:177
  56.1 1.4 convolution_add_fusion.2
  57.5 1.4 fusion.76
  60.6 7.5 %add_reduce_fusion.2 = (f32[816]{0:T(1024)S(1)}, f32[816,4096]{1,0:T(8,128)S(1)}) fusion(f32[4096]{0:T(1024)S(1)} %convert_element_type.65, bf16[816,640]{1,0:T(8,128)(2,1)S(1)} %convert_element_type.64, bf16[640,4096]{1,0:T(8,128)(2,1)} %get-tuple-element.1149), kind=kOutput, calls=%fused_computation.66.clone.1 | convolution fusion | flops 4284873984 | bytes 19676352 | tf_op jit(solution)/shard_map/while/body/eval_jaxpr/dot_general | solution.py:114
  68.1 2.3 exponential_reduce_fusion.2
  70.5 2.5 copy-done.1
  73.2 12.7 %select_reduce_fusion.2 = (f32[816]{0:T(1024)S(1)}, f32[816,4096]{1,0:T(8,128)}) fusion(s32[816]{0:T(1024)S(1)} %eq.178, f32[816]{0:T(1024)S(1)} %log.11, f32[816]{0:T(1024)S(1)} %get-tuple-element.1059, f32[816,4096]{1,0:T(8,128)} %copy-done.1, f32[4096]{0:T(1024)S(1)} %convert_element_type.65), kind=kLoop, calls=%fused_computation.62.clone.1 | loop fusion | flops 20053200 | bytes 26768128 | tf_op jit(solution)/shard_map/while/body/eval_jaxpr/reduce_sum | solution.py:120
  85.9 1.2 slice_reduce_fusion.2
  87.3 11.3 %bitcast_dynamic-update-slice_fusion.5 = f32[2,816,4096]{2,1,0:T(8,128)} fusion(f32[2,816,4096]{2,1,0:T(8,128)} %get-tuple-element.1126, s32[]{:T(128)} %get-tuple-element.1124, f32[816,4096]{1,0:T(8,128)} %get-tuple-element.1060), kind=kLoop, calls=%fused_computation.61.clone.1 | loop fusion | bytes 26739200 | tf_op jit(solution)/shard_map/while/body/jit(dynamic_update_index_in_dim)/dynamic_update_slice | solution.py:177
  100.8 12.4 %gather_fusion = f32[1088,2]{1,0:T(8,128)S(1)} fusion(f32[2,48,17]{0,1,2:T(8,128)S(1)} %copy.55, s32[1088]{0:T(1024)S(1)} %reshape.180), kind=kCustom, calls=%fused_computation | custom fusion | bytes 26112 | tf_op jit(solution)/shard_map/gather | solution.py:31
  113.6 12.1 %gather_fusion.1 = f32[1088,2]{1,0:T(8,128)S(1)} fusion(f32[2,48,17]{0,1,2:T(8,128)S(1)} %copy.57, s32[1088]{0:T(1024)S(1)} %reshape.180), kind=kCustom, calls=%fused_computation.1 | custom fusion | bytes 26112 | tf_op jit(solution)/shard_map/gather | solution.py:31
  126.4 106.5 %while.59 = (s32[]{:T(128)}, f32[2,17]{1,0:T(2,128)S(1)}, f32[2,17]{1,0:T(2,128)S(1)}, f32[64,2,17]{2,1,0:T(2,128)S(1)}, f32[64,2,17]{2,1,0:T(2,128)S(1)}, /*ind...) while((s32[]{:T(128)}, f32[2,17]{1,0:T(2,128)S(1)}, ...), condition=%wide.region_6.7_spmd.clone, body=%wide.region_5.6_spmd.clone.sunk | while | flops 1434 | bytes 22799 | solution.py:94
  234.0 9.8 %gather_fusion.2 = f32[816,2]{1,0:T(8,128)S(1)} fusion(f32[2,64,17]{0,1,2:T(8,128)S(1)} %bitcast.183, s32[816]{0:T(1024)S(1)} %reshape.192), kind=kCustom, calls=%fused_computation.2 | custom fusion | bytes 19584 | tf_op jit(solution)/shard_map/gather | solution.py:41
  245.2 9.8 %gather_fusion.4 = f32[816,2]{1,0:T(8,128)S(1)} fusion(f32[2,64,17]{0,1,2:T(8,128)S(1)} %bitcast.185, s32[816]{0:T(1024)S(1)} %reshape.192), kind=kCustom, calls=%fused_computation.4 | custom fusion | bytes 19584 | tf_op jit(solution)/shard_map/gather | solution.py:41
  256.1 9.8 %gather_fusion.3 = f32[816,2]{1,0:T(8,128)S(1)} fusion(f32[2,64,17]{0,1,2:T(8,128)S(1)} %bitcast.184, s32[816]{0:T(1024)S(1)} %reshape.192), kind=kCustom, calls=%fused_computation.3 | custom fusion | bytes 19584 | tf_op jit(solution)/shard_map/gather | solution.py:41
  266.3 99.7 %while.60 = (s32[]{:T(128)}, f32[]{:T(128)}, f32[640,640]{1,0:T(8,128)}, f32[640,640]{1,0:T(8,128)}, f32[640,4096]{1,0:T(8,128)}, /*index=5*/f32[4096]{0:T(1024)...) while((s32[]{:T(128)}, f32[]{:T(128)}, ...), condition=%wide.region_12.13_spmd.clone, body=%wide.region_7.12_spmd.clone.sunk | while | flops 8649718784 | bytes 146314000 | solution.py:193
  277.6 11.2 %fusion.89 = bf16[816,4096]{1,0:T(8,128)(2,1)} fusion(f32[2,816,4096]{2,1,0:T(8,128)} %get-tuple-element.1265, s32[]{:T(128)} %get-tuple-element.1235, f32[816]{0:T(1024)S(1)} %reshape.215, s32[816]{0:T(1024)S(1)} %eq.189, f32[816]{0:T(1024)S(1)} %exp.63, f32[816]{0:T(1024)S(1)} %add.416, pred[4096]{0:T(1024)(128)(4,1)S(1)} %iota_compare_fusion.4), kind=kLoop, calls=%fused_computation.33.clone.1 | loop fusion | flops 23396352 | bytes 20071172 | tf_op jit(solution)/shard_map/while/body/eval_jaxpr/convert_element_type | solution.py:144
  288.8 10.6 %select_add_fusion.12 = f32[640,4096]{1,0:T(8,128)} fusion(f32[640,4096]{1,0:T(8,128)} %get-tuple-element.1239, bf16[816,4096]{1,0:T(8,128)(2,1)} %fusion.89, pred[]{:T(512)S(6)} %compare.12, bf16[2,816,640]{2,1,0:T(8,128)(2,1)} %get-tuple-element.1272, s32[]{:T(128)} %get-tuple-element.1235), kind=kOutput, calls=%fused_computation.36.clone.1 | convolution fusion | flops 4283432960 | bytes 28701184 | tf_op jit(solution)/shard_map/while/body/eval_jaxpr/dot_general | solution.py:145
  299.5 8.1 %subtract_multiply_fusion.2 = f32[816,640]{1,0:T(8,128)} fusion(bf16[816,4096]{1,0:T(8,128)(2,1)S(1)} %copy-done, bf16[640,4096]{1,0:T(8,128)(2,1)S(1)} %bitcast.202, bf16[2,816,640]{2,1,0:T(8,128)(2,1)} %get-tuple-element.1272, s32[]{:T(128)} %get-tuple-element.1235), kind=kOutput, calls=%fused_computation.37.clone.1 | convolution fusion | flops 4280279040 | bytes 15060996 | tf_op jit(solution)/shard_map/while/body/eval_jaxpr/dot_general | solution.py:149
  307.6 3.1 reshape.216
  310.7 2.5 fusion.90
  313.2 1.6 select_add_fusion.11
  314.8 1.6 select_add_fusion.10
  320.8 11.2 %fusion.89 = bf16[816,4096]{1,0:T(8,128)(2,1)} fusion(f32[2,816,4096]{2,1,0:T(8,128)} %get-tuple-element.1265, s32[]{:T(128)} %get-tuple-element.1235, f32[816]{0:T(1024)S(1)} %reshape.215, s32[816]{0:T(1024)S(1)} %eq.189, f32[816]{0:T(1024)S(1)} %exp.63, f32[816]{0:T(1024)S(1)} %add.416, pred[4096]{0:T(1024)(128)(4,1)S(1)} %iota_compare_fusion.4), kind=kLoop, calls=%fused_computation.33.clone.1 | loop fusion | flops 23396352 | bytes 20071172 | tf_op jit(solution)/shard_map/while/body/eval_jaxpr/convert_element_type | solution.py:144
  332.0 12.1 %select_add_fusion.12 = f32[640,4096]{1,0:T(8,128)} fusion(f32[640,4096]{1,0:T(8,128)} %get-tuple-element.1239, bf16[816,4096]{1,0:T(8,128)(2,1)} %fusion.89, pred[]{:T(512)S(6)} %compare.12, bf16[2,816,640]{2,1,0:T(8,128)(2,1)} %get-tuple-element.1272, s32[]{:T(128)} %get-tuple-element.1235), kind=kOutput, calls=%fused_computation.36.clone.1 | convolution fusion | flops 4283432960 | bytes 28701184 | tf_op jit(solution)/shard_map/while/body/eval_jaxpr/dot_general | solution.py:145
  344.4 8.1 %subtract_multiply_fusion.2 = f32[816,640]{1,0:T(8,128)} fusion(bf16[816,4096]{1,0:T(8,128)(2,1)S(1)} %copy-done, bf16[640,4096]{1,0:T(8,128)(2,1)S(1)} %bitcast.202, bf16[2,816,640]{2,1,0:T(8,128)(2,1)} %get-tuple-element.1272, s32[]{:T(128)} %get-tuple-element.1235), kind=kOutput, calls=%fused_computation.37.clone.1 | convolution fusion | flops 4280279040 | bytes 15060996 | tf_op jit(solution)/shard_map/while/body/eval_jaxpr/dot_general | solution.py:149
  352.5 3.1 reshape.216
  355.6 2.5 fusion.90
  358.2 3.0 select_add_fusion.11
  361.2 3.0 select_add_fusion.10
  368.0 10.5 %all-reduce.9 = (f32[]{:T(128)}, f32[]{:T(128)}) all-reduce(f32[]{:T(128)} %get-tuple-element.408, f32[]{:T(128)S(6)} %convert_element_type.42), channel_id=1, replica_groups=mesh['dp_0'=4,'dp_1'=4,'dp_2'=2,'rep'=4] {'dp_0'}, use_global_device_ids=true, to_apply=%region_23.24 | all-reduce | flops 2 | bytes 16 | tf_op jit(solution)/shard_map/psum | solution.py:16
  378.5 10.8 %all-reduce.8 = (f32[]{:T(128)}, f32[]{:T(128)}) all-reduce(f32[]{:T(128)} %get-tuple-element.762, f32[]{:T(128)} %get-tuple-element.763), channel_id=1, replica_groups=mesh['dp_0'=4,'dp_1'=4,'dp_2'=2,'rep'=4] {'dp_1'}, use_global_device_ids=true, to_apply=%region_24.25 | all-reduce | flops 2 | bytes 16 | tf_op jit(solution)/shard_map/psum | solution.py:16
  389.3 7.0 %all-reduce.10 = (f32[]{:T(128)}, f32[]{:T(128)}) all-reduce(f32[]{:T(128)} %get-tuple-element.760, f32[]{:T(128)} %get-tuple-element.761), channel_id=1, replica_groups=mesh['dp_0'=4,'dp_1'=4,'dp_2'=2,'rep'=4] {'dp_2'}, use_global_device_ids=true, to_apply=%region_25.26 | all-reduce | flops 2 | bytes 16 | tf_op jit(solution)/shard_map/psum | solution.py:16
  396.3 10.1 %all-reduce.7 = (f32[]{:T(128)}, f32[]{:T(128)}) all-reduce(f32[]{:T(128)} %get-tuple-element.764, f32[]{:T(128)} %get-tuple-element.765), channel_id=1, replica_groups=mesh['dp_0'=4,'dp_1'=4,'dp_2'=2,'rep'=4] {'rep'}, use_global_device_ids=true, to_apply=%region_26.27 | all-reduce | flops 2 | bytes 16 | tf_op jit(solution)/shard_map/psum | solution.py:16
  407.8 63.5 %all-reduce.5 = (f32[4096]{0:T(1024)S(1)}, f32[640]{0:T(1024)S(1)}) all-reduce(f32[4096]{0:T(1024)S(1)} %get-tuple-element.406, f32[640]{0:T(1024)S(1)} %get-tuple-element.407), channel_id=1, replica_groups=mesh['dp_0'=4,'dp_1'=4,'dp_2'=2,'rep'=4] {'dp_0','dp_1','dp_2','rep'}, use_global_device_ids=true, to_apply=%region_19.20 | all-reduce | flops 4736 | bytes 37888 | tf_op jit(solution)/shard_map/psum | solution.py:215
  472.5 69.0 %all-reduce.13.cloned.1.call-done = (f32[640,640]{1,0:T(8,128)}, f32[640,640]{1,0:T(8,128)}, f32[640,4096]{1,0:T(8,128)}) async-done(((f32[640,640]{1,0:T(8,128)}, f32[640,640]{1,0:T(8,128)}, f32[640,4096]{1,0:T(8,128)}), (f32[640,640]{1,0:T(8,128)}, f32[640,640]{1,0:T(8,128)}, f32[640,4096]{1,0:T(8,128)})) %all-reduce.13.cloned.1.call-update) | async-done | bytes 13762576 | tf_op jit(solution)/shard_map/psum | solution.py:215
  541.5 7.4 %multiply_reduce_fusion = f32[]{:T(128)} fusion(f32[640,4096]{1,0:T(8,128)} %get-tuple-element.757), kind=kLoop, calls=%fused_computation.83 | loop fusion | flops 5242879 | bytes 10485764 | tf_op jit(solution)/shard_map/reduce_sum | solution.py:204
  554.3 9.7 %broadcast_multiply_fusion = f32[640,4096]{1,0:T(8,128)} fusion(f32[640,4096]{1,0:T(8,128)} %get-tuple-element.757, f32[]{:T(128)S(6)} %rsqrt.3), kind=kLoop, calls=%fused_computation.84 | loop fusion | flops 2621440 | bytes 20971524 | tf_op jit(solution)/shard_map/mul | solution.py:217
  564.0 1.3 broadcast_multiply_fusion.1
  565.3 1.3 broadcast_multiply_fusion.2
  (953 shorter events, 90.3 us)
Async XLA Ops:
  7.2 534.3 %all-reduce.13.cloned.1.call-start = ((), (), s32[]{:S(2)}) async-start(), calls=%async_computation | async-start | bytes 27525120 | tf_op jit(solution)/shard_map/psum | solution.py:215
  11.0 89.7 %copy-start.5 = (s32[64,17,1]{1,0,2:T(8,128)S(1)}, s32[64,17,1]{1,0,2:T(8,128)}, u32[]{:S(2)}) copy-start(s32[64,17,1]{1,0,2:T(8,128)} %fusion.34) | copy-start | bytes 13060
  11.0 115.1 %copy-start.14 = (pred[64,17]{1,0:T(8,128)(4,1)S(1)}, pred[64,17]{1,0:T(8,128)(4,1)}, u32[]{:S(2)}) copy-start(pred[64,17]{1,0:T(8,128)(4,1)} %compare_and_fusion) | copy-start | bytes 3268
  11.0 115.2 %copy-start.6 = (s32[64,17]{1,0:T(8,128)S(1)}, s32[64,17]{1,0:T(8,128)}, u32[]{:S(2)}) copy-start(s32[64,17]{1,0:T(8,128)} %iota_subtract_fusion) | copy-start | bytes 13060
  11.0 115.2 %copy-start.16 = (f32[17]{0:T(128)S(1)}, f32[17]{0:T(128)}, u32[]{:S(2)}) copy-start(f32[17]{0:T(128)} %compare_select_fusion.7) | copy-start | bytes 208
  11.1 115.3 %copy-start.7 = (s32[2]{0:T(128)S(1)}, s32[2]{0:T(128)}, u32[]{:S(2)}) copy-start(s32[2]{0:T(128)} %param.20) | copy-start | bytes 28
  11.1 115.3 %copy-start.10 = (f32[64,2,17]{2,1,0:T(2,128)S(1)}, f32[64,2,17]{2,1,0:T(2,128)}, u32[]{:S(2)}) copy-start(f32[64,2,17]{2,1,0:T(2,128)} %custom-call.20) | copy-start | bytes 26116
  11.1 115.3 %copy-start.11 = (f32[64,2,17]{2,1,0:T(2,128)S(1)}, f32[64,2,17]{2,1,0:T(2,128)}, u32[]{:S(2)}) copy-start(f32[64,2,17]{2,1,0:T(2,128)} %custom-call.21) | copy-start | bytes 26116
  11.1 115.3 %copy-start.12 = (f32[64,2,17]{2,1,0:T(2,128)S(1)}, f32[64,2,17]{2,1,0:T(2,128)}, u32[]{:S(2)}) copy-start(f32[64,2,17]{2,1,0:T(2,128)} %custom-call.22) | copy-start | bytes 26116
  11.1 115.3 %copy-start.13 = (s32[2]{0:T(128)S(1)}, s32[2]{0:T(128)}, u32[]{:S(2)}) copy-start(s32[2]{0:T(128)} %param.19) | copy-start | bytes 28
  11.1 115.3 %copy-start.15 = (f32[2,17]{1,0:T(2,128)S(1)}, f32[2,17]{1,0:T(2,128)}, u32[]{:S(2)}) copy-start(f32[2,17]{1,0:T(2,128)} %custom-call.10) | copy-start | bytes 412
  23.9 4.8 copy-start.1
  23.9 4.8 copy-start.17
  68.1 4.8 copy-start.1
  68.1 4.8 copy-start.17
  99.7 134.2 %copy-start.9 = (s32[48,17,1]{1,0,2:T(8,128)S(1)}, s32[48,17,1]{1,0,2:T(8,128)}, u32[]{:S(2)}) copy-start(s32[48,17,1]{1,0,2:T(8,128)} %fusion.37) | copy-start | bytes 9796
  113.2 153.1 %copy-start.4 = (bf16[2,48,640]{2,1,0:T(8,128)(2,1)S(1)}, bf16[2,48,640]{2,1,0:T(8,128)(2,1)}, u32[]{:S(2)}) copy-start(bf16[2,48,640]{2,1,0:T(8,128)(2,1)} %get-tuple-element.1290) | copy-start | bytes 368644
  113.3 153.1 %copy-start.18 = (s32[2,16]{1,0:T(2,128)S(1)}, s32[2,16]{1,0:T(2,128)}, u32[]{:S(2)}) copy-start(s32[2,16]{1,0:T(2,128)} %get-tuple-element.1294) | copy-start | bytes 388
  277.6 21.8 %slice-start.2 = ((s8[5242880]{0:T(1024)(128)(4,1)}), s8[1048576]{0:T(1024)(128)(4,1)S(1)}, s32[]{:S(2)}) async-start(s8[5242880]{0:T(1024)(128)(4,1)} %bitcast.201), calls=%async_computation.3 | async-start | bytes 2097152 | tf_op jit(solution)/shard_map/while
  288.8 10.6 %copy-start = (bf16[816,4096]{1,0:T(8,128)(2,1)S(1)}, bf16[816,4096]{1,0:T(8,128)(2,1)}, u32[]{:S(2)}) copy-start(bf16[816,4096]{1,0:T(8,128)(2,1)} %fusion.89) | copy-start | bytes 20054020 | tf_op jit(solution)/shard_map/while
  288.8 10.6 %slice-start.3 = ((s8[5242880]{0:T(1024)(128)(4,1)}), s8[4194304]{0:T(1024)(128)(4,1)S(1)}, s32[]{:S(2)}) async-start(s8[5242880]{0:T(1024)(128)(4,1)} %bitcast.201), calls=%async_computation.4 | async-start | bytes 8388608 | tf_op jit(solution)/shard_map/while
  307.6 8.8 %slice-start = ((s8[6684672]{0:T(1024)(128)(4,1)}), s8[2490368]{0:T(1024)(128)(4,1)S(1)}, s32[]{:S(2)}) async-start(s8[6684672]{0:T(1024)(128)(4,1)} %bitcast.181), calls=%async_computation.1 | async-start | bytes 4980736 | tf_op jit(solution)/shard_map/while
  310.7 5.7 slice-start.1
  320.8 23.3 %slice-start.2 = ((s8[5242880]{0:T(1024)(128)(4,1)}), s8[1048576]{0:T(1024)(128)(4,1)S(1)}, s32[]{:S(2)}) async-start(s8[5242880]{0:T(1024)(128)(4,1)} %bitcast.201), calls=%async_computation.3 | async-start | bytes 2097152 | tf_op jit(solution)/shard_map/while
  332.0 12.1 %copy-start = (bf16[816,4096]{1,0:T(8,128)(2,1)S(1)}, bf16[816,4096]{1,0:T(8,128)(2,1)}, u32[]{:S(2)}) copy-start(bf16[816,4096]{1,0:T(8,128)(2,1)} %fusion.89) | copy-start | bytes 20054020 | tf_op jit(solution)/shard_map/while
  332.0 12.4 %slice-start.3 = ((s8[5242880]{0:T(1024)(128)(4,1)}), s8[4194304]{0:T(1024)(128)(4,1)S(1)}, s32[]{:S(2)}) async-start(s8[5242880]{0:T(1024)(128)(4,1)} %bitcast.201), calls=%async_computation.4 | async-start | bytes 8388608 | tf_op jit(solution)/shard_map/while
  352.5 11.7 %slice-start = ((s8[6684672]{0:T(1024)(128)(4,1)}), s8[2490368]{0:T(1024)(128)(4,1)S(1)}, s32[]{:S(2)}) async-start(s8[6684672]{0:T(1024)(128)(4,1)} %bitcast.181), calls=%async_computation.1 | async-start | bytes 4980736 | tf_op jit(solution)/shard_map/while
  355.6 8.6 %slice-start.1 = ((s8[6684672]{0:T(1024)(128)(4,1)}), s8[4194304]{0:T(1024)(128)(4,1)S(1)}, s32[]{:S(2)}) async-start(s8[6684672]{0:T(1024)(128)(4,1)} %bitcast.181), calls=%async_computation.2 | async-start | bytes 8388608 | tf_op jit(solution)/shard_map/while
  366.0 0.7 copy-start.8
  541.5 7.4 %copy-start.2 = (f32[640,640]{1,0:T(8,128)S(1)}, f32[640,640]{1,0:T(8,128)}, u32[]{:S(2)}) copy-start(f32[640,640]{1,0:T(8,128)} %get-tuple-element.755) | copy-start | bytes 4915204
  541.5 7.4 %copy-start.3 = (f32[640,640]{1,0:T(8,128)S(1)}, f32[640,640]{1,0:T(8,128)}, u32[]{:S(2)}) copy-start(f32[640,640]{1,0:T(8,128)} %get-tuple-element.756) | copy-start | bytes 4915204
Sparse Core Ops, SparseCore 0:
  366.2 175.2 all-reduce.12
where the time goes:
time: 580 us; the launch traced here: 575 us
  local copies, waits for them, and re-layouts  149 us (26%)
  other arithmetic  109 us (19%)
  blocking collectives  102 us (18%)
  waiting for transfers between devices  69 us (12%)
  matrix products  68.8 us (12%)
  loops' own time  56.6 us (10%)
  between operations  21 us (4%)
    psum x1, waiting for transfers between devices, per_device(): lax.psum((grads[0], grads[1], grads[2], grads[3], grads[4]), DP_REP)  69 us
    psum x1, blocking collectives, per_device(): lax.psum((grads[0], grads[1], grads[2], grads[3], grads[4]), DP_REP)  63.5 us
    another operation x1, loops' own time, lattice(): lax.scan(both_ways, (first_diag, neg_grid), inputs)  46.1 us
    dynamic_slice x256, local copies, waits for them, and re-layouts, lattice(): lax.scan(both_ways, (first_diag, neg_grid), inputs)  39.8 us
    psum x4, blocking collectives, by_axis(): value = lax.psum(value, axis)  38.4 us
    gather x9, local copies, waits for them, and re-layouts, unskewed(): by_utterance[:, frame_ids[:, None] + positions[None, :], positions[None, :]]  30.3 us
    reduce_sum x2, other arithmetic, joint_forward(): jnp.sum(jnp.where(is_target, log_probs, 0.0), axis=1)  25.4 us
    gather x6, local copies, waits for them, and re-layouts, skewed(): grid[:, jnp.clip(frame_index, 0, num_frames - 1), positions[None, :]]  25.3 us
  transfers between devices with their start and end apart: 1, of which 1 were waited for; matrix products, arithmetic and copies ran while one was open for 0% of the time, Pallas kernels for 0%

commit v1 on v0

v1 whole, which is shorter than its diff:
```python
import functools

import jax
import jax.numpy as jnp
from jax import lax
from jax.experimental import pallas as pl
from jax.experimental.pallas import tpu as pltpu
from jax.sharding import PartitionSpec as P

AXES = ("dp", "rep")
NEG = -1e30
EPS = 1e-06
F32 = jnp.float32
BF16 = jnp.bfloat16
LANES = 128
SLOT = 32
CHUNK = 512
ROWS = 416


def local_kernel(
    labels_ref, frame_ref, label_ref, enc_ref, pred_ref, w_enc_ref, w_pred_ref, b_joint_ref, w_out_ref, b_out_ref,
    g_out_ref, g_side_ref,
    hid, hid_t, logits, dhid, dlog, top, tot, lse, occ, emit_occ, blank_occ, target, blank_d, emit_d, alpha_d,
    beta_d, below_d, right_d, pred_pad, dpred_pad, denc, g_buf, bias_acc, sems,
):
    utts, frames, _ = enc_ref.shape
    slots = pred_ref.shape[1]
    width = w_enc_ref.shape[1]
    vocab = w_out_ref.shape[1]
    rows_all = hid.shape[0]
    cells = utts * slots * frames
    diags = frames + slots - 1
    blocks = [(i, u, (i * slots + u) * frames, SLOT * i + u) for i in range(utts) for u in range(slots)]
    lane_row = lax.broadcasted_iota(jnp.int32, (1, LANES), 1)
    lane_cell = lax.broadcasted_iota(jnp.int32, (frames, LANES), 1)

    def label_at(i, u):
        return labels_ref[i, u] if u < slots - 1 else 1

    pred_pad[...] = jnp.zeros_like(pred_pad)
    hid[cells:, :] = jnp.zeros((rows_all - cells, width), BF16)
    enc_proj = [jnp.dot(enc_ref[i], w_enc_ref[...], preferred_element_type=F32) for i in range(utts)]
    for i in range(utts):
        pred_pad[SLOT * i : SLOT * i + slots, :] = pred_ref[i]
    pred_proj = jnp.dot(pred_pad[...], w_pred_ref[...], preferred_element_type=F32) + b_joint_ref[...].astype(F32)
    for i, u, row, col in blocks:
        hid[row : row + frames, :] = jnp.tanh(enc_proj[i] + pred_proj[col : col + 1, :]).astype(BF16)
    hid_t[...] = hid[...].T

    label_row = jnp.full((1, LANES), -1, jnp.int32)
    for i, u, row, col in blocks:
        label_row = jnp.where(lane_row == col, label_at(i, u), label_row)
    picks = lax.broadcasted_iota(jnp.int32, (vocab, LANES), 0) == label_row
    picks = picks.astype(F32).astype(BF16)
    w_pick = jnp.dot(w_out_ref[...], picks, preferred_element_type=F32).astype(BF16)
    b_pick = jnp.dot(
        jnp.broadcast_to(b_out_ref[...], (16, vocab)), picks, preferred_element_type=F32
    )[:1, :]
    w_blank = jnp.broadcast_to(w_out_ref[:, :1].astype(F32), (width, LANES)).astype(BF16)
    w_two = jnp.concatenate([w_pick, w_blank], axis=1)
    b_blank = b_out_ref[:, :1].astype(F32)

    top[...] = jnp.full_like(top, NEG)
    tot[...] = jnp.zeros_like(tot)

    def forward(c, carry):
        cols = pl.ds(pl.multiple_of(c * CHUNK, CHUNK), CHUNK)
        w_c = w_out_ref[:, cols]
        b_c = b_out_ref[:, cols].astype(F32)
        for r in range(0, rows_all, ROWS):
            z = jnp.dot(hid[r : r + ROWS, :], w_c, preferred_element_type=F32) + b_c
            logits[r : r + ROWS, cols] = z
            tiles = [z[:, k : k + LANES] for k in range(0, CHUNK, LANES)]
            old = top[r : r + ROWS, :]
            new = functools.reduce(jnp.maximum, tiles, old)
            top[r : r + ROWS, :] = new
            tot[r : r + ROWS, :] = tot[r : r + ROWS, :] * jnp.exp(old - new) + sum(jnp.exp(t - new) for t in tiles)
        return carry

    lax.fori_loop(0, vocab // CHUNK, forward, 0)

    for r in range(0, rows_all, ROWS):
        row_top = jnp.max(top[r : r + ROWS, :], axis=1, keepdims=True)
        row_sum = jnp.sum(tot[r : r + ROWS, :] * jnp.exp(top[r : r + ROWS, :] - row_top), axis=1, keepdims=True)
        row_lse = jnp.broadcast_to(row_top + jnp.log(row_sum), (ROWS, LANES))
        lse[r : r + ROWS, :] = row_lse
        two = jnp.dot(hid[r : r + ROWS, :], w_two, preferred_element_type=F32)
        top[r : r + ROWS, :] = two[:, :LANES] + b_pick - row_lse
        tot[r : r + ROWS, :] = two[:, LANES:] + b_blank - row_lse

    blank_d[...] = jnp.full_like(blank_d, NEG)
    emit_d[...] = jnp.full_like(emit_d, NEG)
    for i, u, row, col in blocks:
        here = lane_cell == col
        emit_d[u : u + frames, :] = jnp.where(here, top[row : row + frames, :], emit_d[u : u + frames, :])
        blank_d[u : u + frames, :] = jnp.where(here, tot[row : row + frames, :], blank_d[u : u + frames, :])
    label_pos = lax.rem(lane_row, SLOT)
    frame_count = jnp.full((1, LANES), 0, jnp.int32)
    label_count = jnp.full((1, LANES), -1, jnp.int32)
    for i in range(utts):
        mine = lane_row // SLOT == i
        frame_count = jnp.where(mine, frame_ref[i], frame_count)
        label_count = jnp.where(mine, label_ref[i], label_count)

    def join(a, b):
        hi = jnp.maximum(a, b)
        return hi + jnp.log(1.0 + jnp.exp(jnp.minimum(a, b) - hi))

    alpha = jnp.where((label_pos == 0) & (lane_row < SLOT * utts), 0.0, NEG).astype(F32)
    beta = jnp.full((1, LANES), NEG, F32)
    alpha_d[0:1, :] = alpha
    for step in range(diags):
        d = diags - 1 - step
        t = d - label_pos
        live = (t >= 0) & (t < frame_count) & (label_pos <= label_count)
        last = (t == frame_count - 1) & (label_pos == label_count)
        below = jnp.where(last, 0.0, beta)
        right = pltpu.roll(beta, LANES - 1, 1)
        below_d[d : d + 1, :] = below
        right_d[d : d + 1, :] = right
        beta = jnp.where(live, join(below + blank_d[d : d + 1, :], right + emit_d[d : d + 1, :]), NEG)
        beta_d[d : d + 1, :] = beta
        if step > 0:
            left = pltpu.roll(alpha + emit_d[step - 1 : step, :], 1, 1)
            alpha = join(alpha + blank_d[step - 1 : step, :], left)
            alpha_d[step : step + 1, :] = alpha
    total = jnp.full((1, LANES), 0.0, F32)
    for i in range(utts):
        beta_0 = jnp.sum(jnp.where(lane_row == SLOT * i, beta, 0.0), axis=1, keepdims=True)
        total = jnp.where(lane_row // SLOT == i, beta_0, total)
    span = slice(0, diags)
    blank_d[span, :] = jnp.exp(
        jnp.minimum(alpha_d[span, :] + blank_d[span, :] + below_d[span, :] - total, 80.0)
    )
    emit_d[span, :] = jnp.exp(jnp.minimum(alpha_d[span, :] + emit_d[span, :] + right_d[span, :] - total, 80.0))

    pad = slice(cells, rows_all)
    occ[pad, :] = jnp.zeros((rows_all - cells, LANES), F32)
    emit_occ[pad, :] = jnp.zeros((rows_all - cells, LANES), F32)
    blank_occ[pad, :] = jnp.zeros((rows_all - cells, LANES), F32)
    target[pad, :] = jnp.full((rows_all - cells, LANES), -1, jnp.int32)
    for i, u, row, col in blocks:
        here = slice(row, row + frames)
        b = jnp.broadcast_to(blank_d[u : u + frames, col : col + 1], (frames, LANES))
        e = jnp.broadcast_to(emit_d[u : u + frames, col : col + 1], (frames, LANES))
        blank_occ[here, :] = b
        emit_occ[here, :] = e
        occ[here, :] = b + e
        target[here, :] = jnp.full((frames, LANES), label_at(i, u), jnp.int32)

    dhid[...] = jnp.zeros_like(dhid)

    def out_copy(c, slot):
        cols = pl.ds(pl.multiple_of(c * CHUNK, CHUNK), CHUNK)
        return pltpu.make_async_copy(g_buf.at[slot], g_out_ref.at[:, cols], sems.at[slot])

    def backward(c, carry):
        cols = pl.ds(pl.multiple_of(c * CHUNK, CHUNK), CHUNK)
        slot = lax.rem(c, 2)
        w_c = w_out_ref[:, cols]
        first = c == 0
        for r in range(0, rows_all, ROWS):
            here = slice(r, r + ROWS)
            row_lse, row_occ, row_emit = lse[here, :], occ[here, :], emit_occ[here, :]
            row_target = target[here, :] - c * CHUNK
            lane = lax.broadcasted_iota(jnp.int32, (ROWS, LANES), 1)
            for k in range(0, CHUNK, LANES):
                z = logits[here, pl.ds(pl.multiple_of(c * CHUNK + k, LANES), LANES)]
                d = jnp.exp(z - row_lse) * row_occ - jnp.where(lane + k == row_target, row_emit, 0.0)
                if k == 0:
                    d = d - jnp.where((lane == 0) & first, blank_occ[here, :], 0.0)
                dlog[here, k : k + LANES] = d.astype(BF16)
            dhid[here, :] += lax.dot_general(
                dlog[here, :], w_c, (((1,), (1,)), ((), ())), preferred_element_type=F32
            )

        @pl.when(c >= 2)
        def _():
            out_copy(c - 2, slot).wait()

        g_buf[slot] = jnp.dot(hid_t[...], dlog[...], preferred_element_type=F32)
        bias_acc[:, cols] = jnp.dot(jnp.ones((16, rows_all), BF16), dlog[...], preferred_element_type=F32)[:8, :]
        out_copy(c, slot).start()
        return carry

    steps = vocab // CHUNK
    lax.fori_loop(0, steps, backward, 0)

    dpred_pad[...] = jnp.zeros_like(dpred_pad)
    for i in range(utts):
        enc_sum = jnp.zeros((frames, width), F32)
        for u in range(slots):
            row = (i * slots + u) * frames
            h = hid[row : row + frames, :].astype(F32)
            dpre = dhid[row : row + frames, :] * (1.0 - h * h)
            enc_sum = enc_sum + dpre
            dpred_pad[SLOT * i + u : SLOT * i + u + 1, :] = jnp.sum(dpre, axis=0, keepdims=True)
        denc[i] = enc_sum.astype(BF16)
    dpred = dpred_pad[...].astype(BF16)
    over_rows = (((0,), (0,)), ((), ()))
    g_enc = jnp.zeros((width, width), F32)
    for i in range(utts):
        g_enc = g_enc + lax.dot_general(enc_ref[i], denc[i], over_rows, preferred_element_type=F32)
    g_side_ref[0:width, :] = g_enc
    g_side_ref[width : 2 * width, :] = lax.dot_general(pred_pad[...], dpred, over_rows, preferred_element_type=F32)
    at = 2 * width
    g_side_ref[at:, :] = jnp.zeros((g_side_ref.shape[0] - at, width), F32)
    g_side_ref[at : at + 1, :] = jnp.sum(dpred.astype(F32), axis=0, keepdims=True)
    for k in range(0, vocab, width):
        n = min(width, vocab - k)
        at += 1
        g_side_ref[at : at + 1, 0:n] = bias_acc[0:1, k : k + n]
    head = (lax.rem(lane_row, SLOT) == 0) & (lane_row < SLOT * utts)
    g_side_ref[at + 1 : at + 2, 0:LANES] = jnp.where(head, -beta_d[0:1, :], 0.0)
    g_side_ref[at + 2 : at + 3, 0:LANES] = jnp.where(head, label_count.astype(F32), 0.0)
    for c in range(max(0, steps - 2), steps):
        out_copy(c, c % 2).wait()


def side_rows(width, vocab):
    return 2 * width + 1 + -(-vocab // width) + 2


def local_grads(enc, pred, labels, frame_len, label_len, w_enc, w_pred, b_joint, w_out, b_out):
    utts, frames, enc_dim = enc.shape
    slots, pred_dim = pred.shape[1:]
    width, vocab = w_out.shape
    rows_all = -(-utts * slots * frames // ROWS) * ROWS
    diags = frames + slots
    diag_rows = -(-diags // 8) * 8
    n_side = -(-side_rows(width, vocab) // 16) * 16
    smem = pl.BlockSpec(memory_space=pltpu.SMEM)
    vmem = pl.BlockSpec(memory_space=pltpu.VMEM)
    cell = lambda t: pltpu.VMEM((rows_all, LANES), t)
    diag = pltpu.VMEM((diag_rows, LANES), F32)
    return pl.pallas_call(
        local_kernel,
        out_shape=(jax.ShapeDtypeStruct((width, vocab), F32), jax.ShapeDtypeStruct((n_side, width), F32)),
        in_specs=[smem] * 3 + [vmem] * 7,
        out_specs=(pl.BlockSpec(memory_space=pl.ANY), vmem),
        scratch_shapes=[
            pltpu.VMEM((rows_all, width), BF16),
            pltpu.VMEM((width, rows_all), BF16),
            pltpu.VMEM((rows_all, vocab), F32),
            pltpu.VMEM((rows_all, width), F32),
            pltpu.VMEM((rows_all, CHUNK), BF16),
            cell(F32), cell(F32), cell(F32), cell(F32), cell(F32), cell(F32), cell(jnp.int32),
            diag, diag, diag, diag, diag, diag,
            pltpu.VMEM((SLOT * utts, pred_dim), BF16),
            pltpu.VMEM((SLOT * utts, width), F32),
            pltpu.VMEM((utts, frames, width), BF16),
            pltpu.VMEM((2, width, CHUNK), F32),
            pltpu.VMEM((8, vocab), F32),
            pltpu.SemaphoreType.DMA((2,)),
        ],
        compiler_params=pltpu.CompilerParams(vmem_limit_bytes=66_000_000),
        name="local_grads",
    )(labels, frame_len, label_len, enc, pred, w_enc, w_pred, b_joint.reshape(1, width), w_out, b_out.reshape(1, vocab))


def per_device(enc, pred, labels, frame_len, label_len, w_enc, w_pred, b_joint, w_out, b_out):
    width, vocab = w_out.shape
    g_out, g_side = local_grads(enc, pred, labels, frame_len, label_len, w_enc, w_pred, b_joint, w_out, b_out)
    g_out, g_side = lax.psum((g_out, g_side), AXES)
    at = 2 * width
    bias_rows = -(-vocab // width)
    grads = g_side[: at + 1 + bias_rows, :]
    squares = jnp.sum(g_out * g_out) + jnp.sum(grads * grads)
    count = w_enc.size + w_pred.size + w_out.size + b_out.size + b_joint.size
    scale = lax.rsqrt(squares / jnp.float32(count) + EPS)
    g_side_scaled = grads * scale
    bias_out = g_side_scaled[at + 1 :, :].reshape(-1)[:vocab]
    loss_sum, label_sum = jnp.sum(g_side[at + 1 + bias_rows : at + 3 + bias_rows, :LANES], axis=1)
    return (
        g_side_scaled[:width],
        g_side_scaled[width:at],
        g_out * scale,
        bias_out,
        g_side_scaled[at],
        loss_sum / label_sum,
    )


def solution(mesh):
    split = P(AXES)
    in_specs = (split, split, split, split, split, P(), P(), P(), P(), P())
    return jax.shard_map(per_device, mesh=mesh, in_specs=in_specs, out_specs=(P(),) * 6, check_vma=False)
```

time: 580 us -> 280 us (0.48)
  local copies, waits for them, and re-layouts: 149 us -> 7.72 us
  waiting for transfers between devices: 69 us -> 175 us
  blocking collectives: 102 us -> 0 us
  other arithmetic: 109 us -> 21.5 us
  matrix products: 68.8 us -> 0 us
  Pallas kernels: 0 us -> 57.1 us
  loops' own time: 56.6 us -> 0 us
    psum x1, waiting for transfers between devices: 69 us -> 175 us  [per_device(): g_out, g_side = lax.psum((g_out, g_side), AXES)]
    psum x5 -> x0, blocking collectives: 102 us -> none  [the longest x1 63.5 us: per_device(): lax.psum((grads[0], grads[1], grads[2], grads[3], grads[4]), DP_REP)]
    dot_general x14 -> x0, matrix products: 68.8 us -> none  [the longest x2 22.7 us: joint_backward(): lax.dot_general(hidden, grad_logits, (((0,), (0,)), ((), ())), preferred_...]
    pallas_call x0 -> x1, Pallas kernels: none -> 57.1 us  [local_grads(): pl.pallas_call(local_kernel, out_shape=(jax.ShapeDtypeStruct((width, voca...]
    another operation x3 -> x0, loops' own time: 56.6 us -> none  [the longest x1 46.1 us: lattice(): lax.scan(both_ways, (first_diag, neg_grid), inputs)]
    gather x15 -> x0, local copies, waits for them, and re-layouts: 55.5 us -> none  [the longest x9 30.3 us: unskewed(): by_utterance[:, frame_ids[:, None] + positions[None, :], positions[None, :]]]
    dynamic_slice x256 -> x0, local copies, waits for them, and re-layouts: 39.8 us -> none  [lattice(): lax.scan(both_ways, (first_diag, neg_grid), inputs)]
    reduce_sum x15 -> x3, other arithmetic: 47.7 us -> 11.4 us  [the longest x2 10.7 us: per_device(): squares = jnp.sum(g_out * g_out) + jnp.sum(grads * grads)]
where the time goes in v1:
time: 280 us
  waiting for transfers between devices  175 us (62%)
  Pallas kernels  57.1 us (20%)
  other arithmetic  21.5 us (8%)
  between operations  17.9 us (6%)
  local copies, waits for them, and re-layouts  7.72 us (3%)
    psum x1, waiting for transfers between devices, per_device(): g_out, g_side = lax.psum((g_out, g_side), AXES)  175 us
    pallas_call x1, Pallas kernels, local_grads(): pl.pallas_call(local_kernel, out_shape=(jax.ShapeDtypeStruct((width, voca...  57.1 us
    reduce_sum x2, other arithmetic, per_device(): squares = jnp.sum(g_out * g_out) + jnp.sum(grads * grads)  10.7 us
    mul x1, other arithmetic, per_device(): g_out * scale  9.83 us
  transfers between devices with their start and end apart: 1, of which 1 were waited for; matrix products, arithmetic and copies ran while one was open for 0% of the time, Pallas kernels for 0%

profile of v1, /device:TPU:1, one launch (start us, length us, event | category | flops | bytes accessed | tf_op | source)
XLA Modules:
  0.0 279.6 jit_solution(150715265059887019)
XLA Ops:
  7.2 0.0 all-reduce.3.cloned.1.call-start
  7.2 1.3 reshape.22.b_joint_ref
  8.5 1.3 reshape.23.b_out_ref
  9.8 1.4 copy.16.pred_ref
  11.2 57.1 %local_grads.1 = (f32[640,4096]{1,0:T(8,128)}, f32[1296,640]{1,0:T(8,128)}) custom-call(s32[2,16]{1,0:T(2,128)} %labels_ref.1, s32[2]{0:T(128)} %frame_ref.1, s32[2]{0:T(128)} %label_ref.1, bf16[2,48,640]{2,1,0:T(8,128)(2,1)} %enc_ref.1, bf16[2,17,640]{2,1,0:T(8,128)(2,1)} %copy.16.pred_ref, bf16[640,640]{1,0:T(8,128)(2,1)} %w_enc_ref.1, ...), custom_call_target="tpu_custom_call" | custom-call | tf_op jit(solution)/shard_map/local_grads/pallas_call | solution.py:237
  68.3 0.0 all-reduce.3.cloned.1.call-update
  68.4 175.3 %all-reduce.3.cloned.1.call-done = (f32[1296,640]{1,0:T(8,128)}, f32[640,4096]{1,0:T(8,128)}) async-done(((f32[1296,640]{1,0:T(8,128)}, f32[640,4096]{1,0:T(8,128)}), (f32[1296,640]{1,0:T(8,128)}, f32[640,4096]{1,0:T(8,128)})) %all-reduce.3.cloned.1.call-update) | async-done | bytes 13803536 | tf_op jit(solution)/shard_map/psum | solution.py:265
  243.7 3.4 %multiply_reduce_fusion.1 = f32[]{:T(128)} fusion(f32[1296,640]{1,0:T(8,128)} %get-tuple-element.10), kind=kLoop, calls=%fused_computation.2 | loop fusion | flops 1648639 | bytes 3297284 | tf_op jit(solution)/shard_map/reduce_sum | solution.py:269
  247.0 0.8 slice_reduce_fusion.1
  247.8 7.3 %multiply_reduce_fusion = f32[]{:T(128)} fusion(f32[640,4096]{1,0:T(8,128)} %get-tuple-element.11), kind=kLoop, calls=%fused_computation | loop fusion | flops 5242879 | bytes 10485764 | tf_op jit(solution)/shard_map/reduce_sum | solution.py:269
  256.4 0.0 copy-start
  256.5 9.8 %broadcast_multiply_fusion = f32[640,4096]{1,0:T(8,128)} fusion(f32[640,4096]{1,0:T(8,128)} %get-tuple-element.11, f32[]{:T(128)S(6)} %rsqrt.3), kind=kLoop, calls=%fused_computation.1 | loop fusion | flops 2621440 | bytes 20971524 | tf_op jit(solution)/shard_map/mul | solution.py:278
  266.3 0.0 copy-done
  266.3 0.2 slice_multiply_fusion
  266.5 0.6 slice_reduce_fusion
  267.1 1.9 fusion
  269.0 0.6 fusion.1
  269.6 0.6 slice.32
  (2 shorter events, 0.0 us)
Async XLA Ops:
  7.2 236.5 %all-reduce.3.cloned.1.call-start = ((), (), s32[]{:S(2)}) async-start(), calls=%async_computation | async-start | bytes 27607040 | tf_op jit(solution)/shard_map/psum | solution.py:265
  256.4 9.8 %copy-start = (f32[1296,640]{1,0:T(8,128)S(1)}, f32[1296,640]{1,0:T(8,128)}, u32[]{:S(2)}) copy-start(f32[1296,640]{1,0:T(8,128)} %get-tuple-element.10) | copy-start | bytes 9953284
Sparse Core Ops, SparseCore 0:
  68.5 175.1 all-reduce.2

commit v2 on v1

--- a/solution.py
+++ b/solution.py
@@ -20,9 +20,9 @@
 
 def local_kernel(
     labels_ref, frame_ref, label_ref, enc_ref, pred_ref, w_enc_ref, w_pred_ref, b_joint_ref, w_out_ref, b_out_ref,
-    g_out_ref, g_side_ref,
+    grads_ref,
     hid, hid_t, logits, dhid, dlog, top, tot, lse, occ, emit_occ, blank_occ, target, blank_d, emit_d, alpha_d,
-    beta_d, below_d, right_d, pred_pad, dpred_pad, denc, g_buf, bias_acc, sems,
+    beta_d, below_d, right_d, pred_pad, dpred_pad, denc, g_buf, bias_acc, g_side, tail, sems, side_sems,
 ):
     utts, frames, _ = enc_ref.shape
     slots = pred_ref.shape[1]
@@ -151,9 +151,15 @@
 
     dhid[...] = jnp.zeros_like(dhid)
 
-    def out_copy(c, slot):
-        cols = pl.ds(pl.multiple_of(c * CHUNK, CHUNK), CHUNK)
-        return pltpu.make_async_copy(g_buf.at[slot], g_out_ref.at[:, cols], sems.at[slot])
+    def out_copies(c, slot):
+        return [
+            pltpu.make_async_copy(
+                g_buf.at[slot, :, pl.ds(k * LANES, LANES)],
+                grads_ref.at[pl.ds(pl.multiple_of((c * (CHUNK // LANES) + k) * width, 8), width), :],
+                sems.at[slot, k],
+            )
+            for k in range(CHUNK // LANES)
+        ]
 
     def backward(c, carry):
         cols = pl.ds(pl.multiple_of(c * CHUNK, CHUNK), CHUNK)
@@ -177,11 +183,13 @@
 
         @pl.when(c >= 2)
         def _():
-            out_copy(c - 2, slot).wait()
+            for copy in out_copies(c - 2, slot):
+                copy.wait()
 
         g_buf[slot] = jnp.dot(hid_t[...], dlog[...], preferred_element_type=F32)
         bias_acc[:, cols] = jnp.dot(jnp.ones((16, rows_all), BF16), dlog[...], preferred_element_type=F32)[:8, :]
-        out_copy(c, slot).start()
+        for copy in out_copies(c, slot):
+            copy.start()
         return carry
 
     steps = vocab // CHUNK
@@ -202,24 +210,49 @@
     g_enc = jnp.zeros((width, width), F32)
     for i in range(utts):
         g_enc = g_enc + lax.dot_general(enc_ref[i], denc[i], over_rows, preferred_element_type=F32)
-    g_side_ref[0:width, :] = g_enc
-    g_side_ref[width : 2 * width, :] = lax.dot_general(pred_pad[...], dpred, over_rows, preferred_element_type=F32)
+    g_side[0:width, :] = g_enc
+    g_side[width : 2 * width, :] = lax.dot_general(pred_pad[...], dpred, over_rows, preferred_element_type=F32)
     at = 2 * width
-    g_side_ref[at:, :] = jnp.zeros((g_side_ref.shape[0] - at, width), F32)
-    g_side_ref[at : at + 1, :] = jnp.sum(dpred.astype(F32), axis=0, keepdims=True)
+    g_side[at:, :] = jnp.zeros((g_side.shape[0] - at, width), F32)
+    g_side[at : at + 1, :] = jnp.sum(dpred.astype(F32), axis=0, keepdims=True)
     for k in range(0, vocab, width):
         n = min(width, vocab - k)
         at += 1
-        g_side_ref[at : at + 1, 0:n] = bias_acc[0:1, k : k + n]
+        g_side[at : at + 1, 0:n] = bias_acc[0:1, k : k + n]
+    tail[...] = jnp.zeros_like(tail)
     head = (lax.rem(lane_row, SLOT) == 0) & (lane_row < SLOT * utts)
-    g_side_ref[at + 1 : at + 2, 0:LANES] = jnp.where(head, -beta_d[0:1, :], 0.0)
-    g_side_ref[at + 2 : at + 3, 0:LANES] = jnp.where(head, label_count.astype(F32), 0.0)
+    tail[0:1, :] = jnp.where(head, -beta_d[0:1, :], 0.0)
+    tail[1:2, :] = jnp.where(head, label_count.astype(F32), 0.0)
+    first = vocab // LANES * width
+    n_side = g_side.shape[0]
+    last_copies = [
+        pltpu.make_async_copy(
+            g_side.at[:, pl.ds(k * LANES, LANES)], grads_ref.at[pl.ds(first + k * n_side, n_side), :], side_sems.at[k]
+        )
+        for k in range(width // LANES)
+    ]
+    first += width // LANES * n_side
+    last_copies.append(
+        pltpu.make_async_copy(tail, grads_ref.at[pl.ds(first, tail.shape[0]), :], side_sems.at[width // LANES])
+    )
+    for copy in last_copies:
+        copy.start()
     for c in range(max(0, steps - 2), steps):
-        out_copy(c, c % 2).wait()
-
-
-def side_rows(width, vocab):
-    return 2 * width + 1 + -(-vocab // width) + 2
+        for copy in out_copies(c, c % 2):
+            copy.wait()
+    for copy in last_copies:
+        copy.wait()
+
+
+UNIT = 512
+
+
+def layout(width, vocab):
+    n_side = -(-(2 * width + 1 + -(-vocab // width)) // 8) * 8
+    used = vocab // LANES * width + width // LANES * n_side
+    units = -(-(used + 8) // (2 * UNIT))
+    parts = [(units + 5 - p) // 6 * UNIT for p in range(6)]
+    return n_side, used, parts
 
 
 def local_grads(enc, pred, labels, frame_len, label_len, w_enc, w_pred, b_joint, w_out, b_out):
@@ -229,16 +262,17 @@
     rows_all = -(-utts * slots * frames // ROWS) * ROWS
     diags = frames + slots
     diag_rows = -(-diags // 8) * 8
-    n_side = -(-side_rows(width, vocab) // 16) * 16
+    n_side, used, parts = layout(width, vocab)
+    n_rows = 2 * sum(parts)
     smem = pl.BlockSpec(memory_space=pltpu.SMEM)
     vmem = pl.BlockSpec(memory_space=pltpu.VMEM)
     cell = lambda t: pltpu.VMEM((rows_all, LANES), t)
     diag = pltpu.VMEM((diag_rows, LANES), F32)
     return pl.pallas_call(
         local_kernel,
-        out_shape=(jax.ShapeDtypeStruct((width, vocab), F32), jax.ShapeDtypeStruct((n_side, width), F32)),
+        out_shape=jax.ShapeDtypeStruct((n_rows, LANES), F32),
         in_specs=[smem] * 3 + [vmem] * 7,
-        out_specs=(pl.BlockSpec(memory_space=pl.ANY), vmem),
+        out_specs=pl.BlockSpec(memory_space=pl.ANY),
         scratch_shapes=[
             pltpu.VMEM((rows_all, width), BF16),
             pltpu.VMEM((width, rows_all), BF16),
@@ -252,34 +286,261 @@
             pltpu.VMEM((utts, frames, width), BF16),
             pltpu.VMEM((2, width, CHUNK), F32),
             pltpu.VMEM((8, vocab), F32),
-            pltpu.SemaphoreType.DMA((2,)),
+            pltpu.VMEM((n_side, width), F32),
+            pltpu.VMEM((n_rows - used, LANES), F32),
+            pltpu.SemaphoreType.DMA((2, CHUNK // LANES)),
+            pltpu.SemaphoreType.DMA((width // LANES + 1,)),
         ],
         compiler_params=pltpu.CompilerParams(vmem_limit_bytes=66_000_000),
         name="local_grads",
     )(labels, frame_len, label_len, enc, pred, w_enc, w_pred, b_joint.reshape(1, width), w_out, b_out.reshape(1, vocab))
 
 
+def exchange_kernel(parts, used, grads_ref, full, squares_ref, data, from_core, arrived, local_sems, send_sems, recv_sems):
+    dp, x = lax.axis_index("dp"), lax.axis_index("rep")
+    core = lax.rem(dp, 2)
+    z = lax.rem(dp // 2, 4)
+    y = dp // 8
+    place = (x, y, z)
+    half_rows = sum(parts)
+    mine, theirs = core * half_rows, (1 - core) * half_rows
+    bases = [sum(parts[:p]) for p in range(6)]
+
+    def device(x, y, z, core):
+        return ((y * 4 + z) * 2 + core, x)
+
+    other_core = device(x, y, z, 1 - core)
+
+    def link(p, s):
+        axis = (p + s) % 3
+        v = place[axis]
+        second = lax.rem((p + s) // 3 + core, 2)
+        peer = second * (3 - v) + (1 - second) * (v + 1 - 2 * lax.rem(v, 2))
+        bit = second * (v // 2) + (1 - second) * lax.rem((v + 1) // 2, 2)
+        where = list(place)
+        where[axis] = peer
+        return device(*where, core), bit
+
+    barrier = pltpu.get_barrier_semaphore()
+    peers = [other_core] + [link(p, 0)[0] for p in range(6)]
+    for peer in peers:
+        pl.semaphore_signal(barrier, inc=1, device_id=peer, device_id_type=pl.DeviceIdType.MESH)
+    pl.semaphore_wait(barrier, len(peers))
+
+    def rows(start, n):
+        return pl.ds(pl.multiple_of(start, 8), n)
+
+    def send(src, dst, index, peer):
+        copy = pltpu.make_async_remote_copy(
+            src_ref=src, dst_ref=dst, send_sem=send_sems.at[index], recv_sem=recv_sems.at[index],
+            device_id=peer, device_id_type=pl.DeviceIdType.MESH,
+        )
+        copy.start()
+        return copy
+
+    sent = []
+    local, swapped = [], []
+    for p in range(6):
+        here = pl.ds(bases[p], parts[p])
+        swapped.append(
+            send(grads_ref.at[rows(theirs + bases[p], parts[p]), :], from_core.at[here, :], p, other_core)
+        )
+        copy = pltpu.make_async_copy(
+            grads_ref.at[rows(mine + bases[p], parts[p]), :], data.at[here, :], local_sems.at[p]
+        )
+        copy.start()
+        local.append(copy)
+    sent += swapped
+
+    offset = list(bases)
+    slots = [0] * 6
+    landing = {}
+    at = 0
+    for p in range(6):
+        for s in range(6):
+            landing[p, s] = at
+            at += parts[p] >> (s + 1)
+    steps = {}
+
+    def start_reduce(p, s):
+        peer, bit = link(p, s)
+        n = parts[p] >> (s + 1)
+        steps[p, s] = send(
+            data.at[rows(offset[p] + (1 - bit) * n, n), :], arrived.at[pl.ds(landing[p, s], n), :], 6 + 6 * s + p, peer
+        )
+        offset[p] = offset[p] + bit * n
+        sent.append(steps[p, s])
+
+    def finish_reduce(p, s):
+        n = parts[p] >> (s + 1)
+        steps[p, s].wait_recv()
+        here = rows(offset[p], n)
+        total = data[here, :] + arrived[pl.ds(landing[p, s], n), :]
+        if s < 5:
+            data[here, :] = total
+        else:
+            full[rows(mine + offset[p], n), :] = total
+
+    for s in range(6):
+        for p in range(6):
+            if s == 0:
+                local[p].wait()
+                swapped[p].wait_recv()
+                here = pl.ds(bases[p], parts[p])
+                data[here, :] += from_core[here, :]
+            else:
+                finish_reduce(p, s - 1)
+            if p > 0:
+                start_reduce(p - 1, s)
+        start_reduce(5, s)
+
+    gathers = {}
+
+    def start_gather(p, s):
+        peer, bit = link(p, s)
+        n = parts[p] >> (s + 1)
+        here = full.at[rows(mine + offset[p], n), :]
+        gathers[p, s] = send(here, here, 42 + 6 * s + p, peer)
+        sent.append(gathers[p, s])
+        if s == 0:
+            give_core(p, offset[p], n, 0)
+            other = bases[p] + (1 - bit) * n
+            gathers[p, "other"] = other
+        offset[p] = offset[p] - bit * n
+
+    crossed = []
+
+    def give_core(p, start, n, which):
+        here = full.at[rows(mine + start, n), :]
+        copy = send(here, here, 78 + 2 * p + which, other_core)
+        crossed.append(copy)
+        sent.append(copy)
+
+    for s in range(5, -1, -1):
+        for p in range(6):
+            if s == 5:
+                finish_reduce(p, 5)
+                if p > 0:
+                    start_gather(p - 1, s)
+            else:
+                gathers[p, s + 1].wait_recv()
+                start_gather(p, s)
+        if s == 5:
+            start_gather(5, s)
+    for p in range(6):
+        gathers[p, 0].wait_recv()
+        give_core(p, gathers[p, "other"], parts[p] >> 1, 1)
+    for copy in crossed:
+        copy.wait_recv()
+
+    block, lines = 960, 64
+
+    def add_squares(k, total):
+        here = full[rows(k * block, block), :].reshape(block // lines, lines, LANES)
+        return total + jnp.sum(here * here, axis=0)
+
+    whole = used // block
+    total = lax.fori_loop(0, whole, add_squares, jnp.zeros((lines, LANES), F32))
+    total = jnp.sum(total.reshape(lines // 8, 8, LANES), axis=0)
+    rest = full[whole * block : used, :].reshape(-1, 8, LANES)
+    squares_ref[...] = total + jnp.sum(rest * rest, axis=0)
+    for copy in sent:
+        copy.wait_send()
+
+
+def exchange(grads, width, vocab):
+    _, used, parts = layout(width, vocab)
+    half_rows = sum(parts)
+    landed = sum(parts[p] >> (s + 1) for p in range(6) for s in range(6))
+    vmem = pl.BlockSpec(memory_space=pltpu.VMEM)
+    return pl.pallas_call(
+        functools.partial(exchange_kernel, parts, used),
+        out_shape=(jax.ShapeDtypeStruct(grads.shape, F32), jax.ShapeDtypeStruct((8, LANES), F32)),
+        in_specs=[pl.BlockSpec(memory_space=pl.ANY)],
+        out_specs=(vmem, vmem),
+        scratch_shapes=[
+            pltpu.VMEM((half_rows, LANES), F32),
+            pltpu.VMEM((half_rows, LANES), F32),
+            pltpu.VMEM((landed, LANES), F32),
+            pltpu.SemaphoreType.DMA((6,)),
+            pltpu.SemaphoreType.DMA((90,)),
+            pltpu.SemaphoreType.DMA((90,)),
+        ],
+        compiler_params=pltpu.CompilerParams(collective_id=0, has_side_effects=True, vmem_limit_bytes=44_000_000),
+        name="exchange",
+    )(grads)
+
+
+def finish_kernel(n_side, used, count, full, squares_ref, out_ref, enc_ref, pred_ref, bias_ref, joint_ref, loss_ref, buf, side_buf, sems):
+    width, vocab = out_ref.shape
+    squares = jnp.sum(jnp.sum(squares_ref[...], axis=0, keepdims=True), axis=1, keepdims=True)
+    scale = lax.rsqrt(squares * (1.0 / count) + EPS)
+    copies = []
+    steps = vocab // CHUNK
+    per = CHUNK // LANES
+    for c in range(steps):
+        slot = c % buf.shape[0]
+        if c >= buf.shape[0]:
+            copies[c - buf.shape[0]].wait()
+        for k in range(per):
+            v = c * per + k
+            buf[slot, :, k * LANES : (k + 1) * LANES] = full[v * width : (v + 1) * width, :] * scale
+        copy = pltpu.make_async_copy(buf.at[slot], out_ref.at[:, pl.ds(c * CHUNK, CHUNK)], sems.at[slot])
+        copy.start()
+        copies.append(copy)
+    first = vocab // LANES * width
+    side_copies = []
+    for i, ref in enumerate((enc_ref, pred_ref)):
+        for k in range(width // LANES):
+            row = first + k * n_side + i * width
+            side_buf[i, :, k * LANES : (k + 1) * LANES] = full[row : row + width, :] * scale
+        copy = pltpu.make_async_copy(side_buf.at[i], ref, sems.at[buf.shape[0] + i])
+        copy.start()
+        side_copies.append(copy)
+    for k in range(width // LANES):
+        row = first + k * n_side + 2 * width
+        joint_ref[:, k * LANES : (k + 1) * LANES] = full[row : row + 1, :] * scale
+        for r in range(-(-vocab // width)):
+            lane = r * width + k * LANES
+            if lane < vocab:
+                bias_ref[:, lane : lane + LANES] = full[row + 1 + r : row + 2 + r, :] * scale
+    loss = jnp.sum(full[used : used + 1, :], axis=1, keepdims=True)
+    labels = jnp.sum(full[used + 1 : used + 2, :], axis=1, keepdims=True)
+    loss_ref[...] = jnp.broadcast_to(loss / labels, loss_ref.shape)
+    for copy in copies[-buf.shape[0] :] + side_copies:
+        copy.wait()
+
+
+def finish(full, squares, width, vocab, count):
+    n_side, used, _ = layout(width, vocab)
+    vmem = pl.BlockSpec(memory_space=pltpu.VMEM)
+    anywhere = pl.BlockSpec(memory_space=pl.ANY)
+    shape = jax.ShapeDtypeStruct
+    return pl.pallas_call(
+        functools.partial(finish_kernel, n_side, used, float(count)),
+        out_shape=(
+            shape((width, vocab), F32), shape((width, width), F32), shape((width, width), F32),
+            shape((1, vocab), F32), shape((1, width), F32), shape((1, LANES), F32),
+        ),
+        in_specs=[vmem, vmem],
+        out_specs=(anywhere, anywhere, anywhere, vmem, vmem, vmem),
+        scratch_shapes=[
+            pltpu.VMEM((4, width, CHUNK), F32),
+            pltpu.VMEM((2, width, width), F32),
+            pltpu.SemaphoreType.DMA((6,)),
+        ],
+        compiler_params=pltpu.CompilerParams(vmem_limit_bytes=40_000_000),
+        name="finish",
+    )(full, squares)
+
+
 def per_device(enc, pred, labels, frame_len, label_len, w_enc, w_pred, b_joint, w_out, b_out):
     width, vocab = w_out.shape
-    g_out, g_side = local_grads(enc, pred, labels, frame_len, label_len, w_enc, w_pred, b_joint, w_out, b_out)
-    g_out, g_side = lax.psum((g_out, g_side), AXES)
-    at = 2 * width
-    bias_rows = -(-vocab // width)
-    grads = g_side[: at + 1 + bias_rows, :]
-    squares = jnp.sum(g_out * g_out) + jnp.sum(grads * grads)
+    grads = local_grads(enc, pred, labels, frame_len, label_len, w_enc, w_pred, b_joint, w_out, b_out)
+    full, squares = exchange(grads, width, vocab)
     count = w_enc.size + w_pred.size + w_out.size + b_out.size + b_joint.size
-    scale = lax.rsqrt(squares / jnp.float32(count) + EPS)
-    g_side_scaled = grads * scale
-    bias_out = g_side_scaled[at + 1 :, :].reshape(-1)[:vocab]
-    loss_sum, label_sum = jnp.sum(g_side[at + 1 + bias_rows : at + 3 + bias_rows, :LANES], axis=1)
-    return (
-        g_side_scaled[:width],
-        g_side_scaled[width:at],
-        g_out * scale,
-        bias_out,
-        g_side_scaled[at],
-        loss_sum / label_sum,
-    )
+    out, g_enc, g_pred, bias, joint, loss = finish(full, squares, width, vocab, count)
+    return g_enc, g_pred, out, bias.reshape(vocab), joint.reshape(width), loss[0, 0]
 
 
 def solution(mesh):

time: 280 us -> 177 us (0.63)
  waiting for transfers between devices: 175 us -> 0 us
  Pallas kernels: 57.1 us -> 167 us
  other arithmetic: 21.5 us -> 0.61 us
  between operations: 17.9 us -> 0.67 us
    psum x1 -> x0, waiting for transfers between devices: 175 us -> none  [per_device(): g_out, g_side = lax.psum((g_out, g_side), AXES)]
    pallas_call x1 -> x3, Pallas kernels: 57.1 us -> 167 us  [the longest x1 104 us: exchange(): pl.pallas_call(functools.partial(exchange_kernel, parts, used), out_shape...]
    reduce_sum x3 -> x0, other arithmetic: 11.4 us -> none  [the longest x2 10.7 us: per_device(): squares = jnp.sum(g_out * g_out) + jnp.sum(grads * grads)]
    mul x2 -> x0, other arithmetic: 10 us -> none  [the longest x1 9.83 us: per_device(): g_out * scale]
    unnamed x3, local copies, waits for them, and re-layouts: 1.42 us -> 6.43 us
    slice x4 -> x0, local copies, waits for them, and re-layouts: 3.13 us -> none  [the longest x1 1.91 us: per_device(): g_side_scaled[width:at]]
  transfers between devices with their start and end apart: 1 -> 0, of which waited for: 1 -> 0; matrix products, arithmetic and copies ran while one was open for 0% -> 0% of each run, Pallas kernels for 0% -> 0%
where the time goes in v2:
time: 177 us
  Pallas kernels  167 us (94%)
  local copies, waits for them, and re-layouts  9.01 us (5%)
    pallas_call x1, Pallas kernels, exchange(): pl.pallas_call(functools.partial(exchange_kernel, parts, used), out_shape...  104 us
    pallas_call x1, Pallas kernels, local_grads(): pl.pallas_call(local_kernel, out_shape=jax.ShapeDtypeStruct((n_rows, LANE...  57.4 us
    unnamed x3, local copies, waits for them, and re-layouts  6.43 us
    pallas_call x1, Pallas kernels, finish(): pl.pallas_call(functools.partial(finish_kernel, n_side, used, float(count...  5.88 us

profile of v2, /device:TPU:1, one launch (start us, length us, event | category | flops | bytes accessed | tf_op | source)
XLA Modules:
  0.0 177.1 jit_solution(1010745827526189810)
XLA Ops:
  0.6 1.3 reshape.24.b_joint_ref
  1.9 1.3 reshape.25.b_out_ref
  3.2 1.4 copy.16.pred_ref
  4.6 57.4 %local_grads.1.grads_ref = f32[27648,128]{1,0:T(8,128)} custom-call(s32[2,16]{1,0:T(2,128)} %labels_ref.1, s32[2]{0:T(128)} %frame_ref.1, s32[2]{0:T(128)} %label_ref.1, bf16[2,48,640]{2,1,0:T(8,128)(2,1)} %enc_ref.1, bf16[2,17,640]{2,1,0:T(8,128)(2,1)} %copy.16.pred_ref, bf16[640,640]{1,0:T(8,128)(2,1)} %w_enc_ref.1, bf16[640,640]{1,0:T(8,128)(2,1)} %w_pred_ref.1, ...), custom_call_target="tpu_custom_call" | custom-call | tf_op jit(solution)/shard_map/local_grads/pallas_call | solution.py:271
  62.0 103.5 %exchange.1 = (f32[27648,128]{1,0:T(8,128)}, f32[8,128]{1,0:T(8,128)S(1)}) custom-call(f32[27648,128]{1,0:T(8,128)} %local_grads.1.grads_ref), custom_call_target="tpu_custom_call" | custom-call | tf_op jit(solution)/shard_map/exchange/pallas_call | solution.py:456
  165.5 0.0 copy-start
  165.5 5.0 %copy-done = f32[27648,128]{1,0:T(8,128)S(1)} copy-done((f32[27648,128]{1,0:T(8,128)S(1)}, f32[27648,128]{1,0:T(8,128)}, u32[]{:S(2)}) %copy-start) | copy-done | bytes 14155800
  170.6 5.9 %finish.1 = (f32[640,4096]{1,0:T(8,128)}, f32[640,640]{1,0:T(8,128)}, f32[640,640]{1,0:T(8,128)}, f32[1,4096]{1,0:T(1,128)}, f32[1,640]{1,0:T(1,128)S(1)}, /*index=5*/f32[1,128]{1,0:T(1,128)}) custom-call(f32[27648,128]{1,0:T(8,128)S(1)} %copy-done, f32[8,128]{1,0:T(8,128)S(1)} %get-tuple-element.15.squares_ref), custom_call_target="tpu_custom_call" | custom-call | tf_op jit(solution)/shard_map/finish/pallas_call | solution.py:519
  176.4 0.6 reduce
Async XLA Ops:
  165.5 5.0 %copy-start = (f32[27648,128]{1,0:T(8,128)S(1)}, f32[27648,128]{1,0:T(8,128)}, u32[]{:S(2)}) copy-start(f32[27648,128]{1,0:T(8,128)} %get-tuple-element.14.full) | copy-start | bytes 42467332

commit v3 on v1

--- a/solution.py
+++ b/solution.py
@@ -19,16 +19,18 @@
 
 
 def local_kernel(
-    labels_ref, frame_ref, label_ref, enc_ref, pred_ref, w_enc_ref, w_pred_ref, b_joint_ref, w_out_ref, b_out_ref,
-    g_out_ref, g_side_ref,
+    labels_ref, frame_ref, label_ref, enc_ref, pred_ref, w_enc_ref, w_pred_ref, b_joint_ref, w_out_hbm, b_out_ref,
+    side_ref, dlog_ref, hid_t_ref,
     hid, hid_t, logits, dhid, dlog, top, tot, lse, occ, emit_occ, blank_occ, target, blank_d, emit_d, alpha_d,
-    beta_d, below_d, right_d, pred_pad, dpred_pad, denc, g_buf, bias_acc, sems,
+    beta_d, below_d, right_d, pred_pad, dpred_pad, denc, bias_acc, slabs, tail, w_out_ref, sems, side_sems, load_sem, hid_sem,
 ):
     utts, frames, _ = enc_ref.shape
     slots = pred_ref.shape[1]
     width = w_enc_ref.shape[1]
     vocab = w_out_ref.shape[1]
     rows_all = hid.shape[0]
+    load = pltpu.make_async_copy(w_out_hbm, w_out_ref, load_sem)
+    load.start()
     cells = utts * slots * frames
     diags = frames + slots - 1
     blocks = [(i, u, (i * slots + u) * frames, SLOT * i + u) for i in range(utts) for u in range(slots)]
@@ -47,6 +49,9 @@
     for i, u, row, col in blocks:
         hid[row : row + frames, :] = jnp.tanh(enc_proj[i] + pred_proj[col : col + 1, :]).astype(BF16)
     hid_t[...] = hid[...].T
+    hid_copy = pltpu.make_async_copy(hid_t, hid_t_ref, hid_sem)
+    hid_copy.start()
+    load.wait()
 
     label_row = jnp.full((1, LANES), -1, jnp.int32)
     for i, u, row, col in blocks:
@@ -151,36 +156,40 @@
 
     dhid[...] = jnp.zeros_like(dhid)
 
+    bias_acc[...] = jnp.zeros_like(bias_acc)
+
     def out_copy(c, slot):
         cols = pl.ds(pl.multiple_of(c * CHUNK, CHUNK), CHUNK)
-        return pltpu.make_async_copy(g_buf.at[slot], g_out_ref.at[:, cols], sems.at[slot])
+        return pltpu.make_async_copy(dlog.at[slot], dlog_ref.at[:, cols], sems.at[slot])
 
     def backward(c, carry):
         cols = pl.ds(pl.multiple_of(c * CHUNK, CHUNK), CHUNK)
         slot = lax.rem(c, 2)
         w_c = w_out_ref[:, cols]
         first = c == 0
+
+        @pl.when(c >= 2)
+        def _():
+            out_copy(c - 2, slot).wait()
+
+        sums = [jnp.zeros((8, LANES), F32)] * (CHUNK // LANES)
         for r in range(0, rows_all, ROWS):
             here = slice(r, r + ROWS)
             row_lse, row_occ, row_emit = lse[here, :], occ[here, :], emit_occ[here, :]
             row_target = target[here, :] - c * CHUNK
             lane = lax.broadcasted_iota(jnp.int32, (ROWS, LANES), 1)
+            parts = []
             for k in range(0, CHUNK, LANES):
                 z = logits[here, pl.ds(pl.multiple_of(c * CHUNK + k, LANES), LANES)]
                 d = jnp.exp(z - row_lse) * row_occ - jnp.where(lane + k == row_target, row_emit, 0.0)
                 if k == 0:
                     d = d - jnp.where((lane == 0) & first, blank_occ[here, :], 0.0)
-                dlog[here, k : k + LANES] = d.astype(BF16)
-            dhid[here, :] += lax.dot_general(
-                dlog[here, :], w_c, (((1,), (1,)), ((), ())), preferred_element_type=F32
-            )
-
-        @pl.when(c >= 2)
-        def _():
-            out_copy(c - 2, slot).wait()
-
-        g_buf[slot] = jnp.dot(hid_t[...], dlog[...], preferred_element_type=F32)
-        bias_acc[:, cols] = jnp.dot(jnp.ones((16, rows_all), BF16), dlog[...], preferred_element_type=F32)[:8, :]
+                sums[k // LANES] = sums[k // LANES] + jnp.sum(d.reshape(ROWS // 8, 8, LANES), axis=0)
+                parts.append(d.astype(BF16))
+            d = jnp.concatenate(parts, axis=1)
+            dlog[slot, here, :] = d
+            dhid[here, :] += lax.dot_general(d, w_c, (((1,), (1,)), ((), ())), preferred_element_type=F32)
+        bias_acc[:, cols] = jnp.concatenate(sums, axis=1)
         out_copy(c, slot).start()
         return carry
 
@@ -202,24 +211,55 @@
     g_enc = jnp.zeros((width, width), F32)
     for i in range(utts):
         g_enc = g_enc + lax.dot_general(enc_ref[i], denc[i], over_rows, preferred_element_type=F32)
-    g_side_ref[0:width, :] = g_enc
-    g_side_ref[width : 2 * width, :] = lax.dot_general(pred_pad[...], dpred, over_rows, preferred_element_type=F32)
-    at = 2 * width
-    g_side_ref[at:, :] = jnp.zeros((g_side_ref.shape[0] - at, width), F32)
-    g_side_ref[at : at + 1, :] = jnp.sum(dpred.astype(F32), axis=0, keepdims=True)
-    for k in range(0, vocab, width):
-        n = min(width, vocab - k)
-        at += 1
-        g_side_ref[at : at + 1, 0:n] = bias_acc[0:1, k : k + n]
+    g_pred = lax.dot_general(pred_pad[...], dpred, over_rows, preferred_element_type=F32)
+    per = width // LANES
+    last_copies = []
+    for i, g in enumerate((g_enc, g_pred)):
+        for k in range(per):
+            slabs[i, k] = g[:, k * LANES : (k + 1) * LANES]
+        for k in range(per):
+            last_copies.append(
+                pltpu.make_async_copy(slabs.at[i, k], side_ref.at[i, pl.ds(k * width, width), :], side_sems.at[i, k])
+            )
+            last_copies[-1].start()
+    tail[...] = jnp.zeros_like(tail)
+    bias = jnp.sum(bias_acc[...], axis=0, keepdims=True)
+    joint = jnp.sum(dpred.astype(F32), axis=0, keepdims=True)
+    for k in range(vocab // LANES):
+        tail[0, k : k + 1, :] = bias[:, k * LANES : (k + 1) * LANES]
+    for k in range(per):
+        tail[0, vocab // LANES + k : vocab // LANES + k + 1, :] = joint[:, k * LANES : (k + 1) * LANES]
     head = (lax.rem(lane_row, SLOT) == 0) & (lane_row < SLOT * utts)
-    g_side_ref[at + 1 : at + 2, 0:LANES] = jnp.where(head, -beta_d[0:1, :], 0.0)
-    g_side_ref[at + 2 : at + 3, 0:LANES] = jnp.where(head, label_count.astype(F32), 0.0)
+    tail[1, 0:1, :] = jnp.where(head, -beta_d[0:1, :], 0.0)
+    tail[1, 1:2, :] = jnp.where(head, label_count.astype(F32), 0.0)
+    for i in range(2):
+        last_copies.append(
+            pltpu.make_async_copy(
+                tail.at[i], side_ref.at[i, pl.ds(per * width, tail.shape[1]), :], side_sems.at[i, per]
+            )
+        )
+        last_copies[-1].start()
     for c in range(max(0, steps - 2), steps):
         out_copy(c, c % 2).wait()
-
-
-def side_rows(width, vocab):
-    return 2 * width + 1 + -(-vocab // width) + 2
+    hid_copy.wait()
+    for copy in last_copies:
+        copy.wait()
+
+
+UNIT = 512
+PER_CHUNK = 5
+BLOCK = 1024
+GAP = 2
+EXTRA = 2
+
+
+def layout(width, vocab):
+    chunks = 1 + vocab // BLOCK
+    main = PER_CHUNK * UNIT
+    half = chunks * main + EXTRA * UNIT
+    per = width // LANES
+    assert main == 4 * width and BLOCK == 8 * LANES and per == 5
+    return chunks, main, half
 
 
 def local_grads(enc, pred, labels, frame_len, label_len, w_enc, w_pred, b_joint, w_out, b_out):
@@ -229,57 +269,342 @@
     rows_all = -(-utts * slots * frames // ROWS) * ROWS
     diags = frames + slots
     diag_rows = -(-diags // 8) * 8
-    n_side = -(-side_rows(width, vocab) // 16) * 16
+    chunks, main, half = layout(width, vocab)
+    side_rows = main + EXTRA * UNIT
+    shape = jax.ShapeDtypeStruct
     smem = pl.BlockSpec(memory_space=pltpu.SMEM)
     vmem = pl.BlockSpec(memory_space=pltpu.VMEM)
+    anywhere = pl.BlockSpec(memory_space=pl.ANY)
     cell = lambda t: pltpu.VMEM((rows_all, LANES), t)
     diag = pltpu.VMEM((diag_rows, LANES), F32)
     return pl.pallas_call(
         local_kernel,
-        out_shape=(jax.ShapeDtypeStruct((width, vocab), F32), jax.ShapeDtypeStruct((n_side, width), F32)),
-        in_specs=[smem] * 3 + [vmem] * 7,
-        out_specs=(pl.BlockSpec(memory_space=pl.ANY), vmem),
+        out_shape=(
+            shape((2, side_rows, LANES), F32), shape((rows_all, vocab), BF16), shape((width, rows_all), BF16),
+        ),
+        in_specs=[smem] * 3 + [vmem] * 5 + [anywhere, vmem],
+        out_specs=(anywhere,) * 3,
         scratch_shapes=[
             pltpu.VMEM((rows_all, width), BF16),
             pltpu.VMEM((width, rows_all), BF16),
             pltpu.VMEM((rows_all, vocab), F32),
             pltpu.VMEM((rows_all, width), F32),
-            pltpu.VMEM((rows_all, CHUNK), BF16),
+            pltpu.VMEM((2, rows_all, CHUNK), BF16),
             cell(F32), cell(F32), cell(F32), cell(F32), cell(F32), cell(F32), cell(jnp.int32),
             diag, diag, diag, diag, diag, diag,
             pltpu.VMEM((SLOT * utts, pred_dim), BF16),
             pltpu.VMEM((SLOT * utts, width), F32),
             pltpu.VMEM((utts, frames, width), BF16),
-            pltpu.VMEM((2, width, CHUNK), F32),
             pltpu.VMEM((8, vocab), F32),
+            pltpu.VMEM((2, width // LANES, width, LANES), F32),
+            pltpu.VMEM((2, side_rows - width // LANES * width, LANES), F32),
+            pltpu.VMEM((width, vocab), BF16),
             pltpu.SemaphoreType.DMA((2,)),
+            pltpu.SemaphoreType.DMA((2, width // LANES + 1)),
+            pltpu.SemaphoreType.DMA(()),
+            pltpu.SemaphoreType.DMA(()),
         ],
         compiler_params=pltpu.CompilerParams(vmem_limit_bytes=66_000_000),
         name="local_grads",
     )(labels, frame_len, label_len, enc, pred, w_enc, w_pred, b_joint.reshape(1, width), w_out, b_out.reshape(1, vocab))
 
 
+def exchange_kernel(
+    chunks, side_ref, dlog_ref, hid_t_ref, full, squares_ref, held, from_core, arrived, d_buf,
+    side_sems, d_sems, core_sems, step_sems, extra_sems,
+):
+    dp, x = lax.axis_index("dp"), lax.axis_index("rep")
+    core = lax.rem(dp, 2)
+    place = (x, dp // 8, lax.rem(dp // 2, 4))
+    width = hid_t_ref.shape[0]
+    extra_at = chunks * PER_CHUNK
+
+    def device(x, y, z, core):
+        return ((y * 4 + z) * 2 + core, x)
+
+    other_core = device(*place, 1 - core)
+
+    def link(turn, s):
+        axis = (turn + s) % 3
+        v = place[axis]
+        second = lax.rem((turn + s) // 3 + core, 2)
+        peer = second * (3 - v) + (1 - second) * (v + 1 - 2 * lax.rem(v, 2))
+        bit = second * (v // 2) + (1 - second) * lax.rem((v + 1) // 2, 2)
+        where = list(place)
+        where[axis] = peer
+        return device(*where, core), bit
+
+    barrier = pltpu.get_barrier_semaphore()
+    peers = [other_core] + [link(p, 0)[0] for p in range(6)]
+    for peer in peers:
+        pl.semaphore_signal(barrier, inc=1, device_id=peer, device_id_type=pl.DeviceIdType.MESH)
+
+    side_copies = []
+    for h in range(2):
+        for n, (src, dst, units) in enumerate(((0, 0, PER_CHUNK), (PER_CHUNK, extra_at, EXTRA))):
+            copy = pltpu.make_async_copy(
+                side_ref.at[h, pl.ds(src, units)], held.at[h, pl.ds(dst, units)], side_sems.at[h, n]
+            )
+            copy.start()
+            side_copies.append(copy)
+
+    def load_block(c):
+        slot = lax.rem(c, 2)
+        cols = pl.ds(pl.multiple_of((c - 1) * BLOCK, BLOCK), BLOCK)
+        return pltpu.make_async_copy(dlog_ref.at[:, cols], d_buf.at[slot], d_sems.at[slot])
+
+    load_block(1).start()
+
+    turns = list(range(PER_CHUNK)) + [5, 2]
+    offsets = []
+    for turn in turns:
+        line = [0]
+        for s in range(6):
+            line.append(line[-1] + link(turn, s)[1] * (UNIT >> (s + 1)))
+        offsets.append(line)
+
+    def rows(start, n):
+        return pl.ds(pl.multiple_of(start, 8), n)
+
+    def remote(src, dst, sems, index, peer):
+        return pltpu.make_async_remote_copy(
+            src_ref=src, dst_ref=dst, send_sem=sems.at[(*index, 0)], recv_sem=sems.at[(*index, 1)],
+            device_id=peer, device_id_type=pl.DeviceIdType.MESH,
+        )
+
+    def unit_of(c, j):
+        return c * PER_CHUNK + j if j < PER_CHUNK else extra_at + j - PER_CHUNK
+
+    def sem_of(c, j, n):
+        return (step_sems, (c, j, n)) if j < PER_CHUNK else (extra_sems, (j - PER_CHUNK, n))
+
+    def swap(c, extra):
+        units = pl.ds(extra_at, EXTRA) if extra else pl.ds(c * PER_CHUNK, PER_CHUNK)
+        return remote(
+            held.at[1 - core, units], from_core.at[units], core_sems, (chunks if extra else c,), other_core
+        )
+
+    def reduce(c, j, s):
+        peer, bit = link(turns[j], s)
+        n = UNIT >> (s + 1)
+        u = unit_of(c, j)
+        return remote(
+            held.at[core, u, rows(offsets[j][s] + (1 - bit) * n, n)],
+            arrived.at[u, pl.ds(UNIT - 2 * n, n)],
+            *sem_of(c, j, s), peer,
+        )
+
+    def add_reduce(c, j, s):
+        n = UNIT >> (s + 1)
+        u = unit_of(c, j)
+        here = rows(offsets[j][s + 1], n)
+        total = held[core, u, here, :] + arrived[u, pl.ds(UNIT - 2 * n, n), :]
+        if s < 5:
+            held[core, u, here, :] = total
+        else:
+            full[core, u, here, :] = total
+
+    def gather(c, j, s):
+        here = full.at[core, unit_of(c, j), rows(offsets[j][s + 1], UNIT >> (s + 1))]
+        return remote(here, here, *sem_of(c, j, 6 + s), link(turns[j], s)[0])
+
+    def give(c, j, late):
+        n = UNIT // 2
+        bit = link(turns[j], 0)[1]
+        start = (1 - bit) * n if late else bit * n
+        here = full.at[core, unit_of(c, j), rows(start, n)]
+        return remote(here, here, *sem_of(c, j, 13 if late else 12), other_core)
+
+    def stage(k, c, lanes):
+        if k == 1:
+            for extra in {j >= PER_CHUNK for j in lanes}:
+                swap(c, extra).wait()
+                units = pl.ds(extra_at, EXTRA) if extra else pl.ds(c * PER_CHUNK, PER_CHUNK)
+                held[core, units] = held[core, units] + from_core[units]
+            for j in lanes:
+                reduce(c, j, 0).start()
+        elif k <= 7:
+            for j in lanes:
+                reduce(c, j, k - 2).wait()
+                add_reduce(c, j, k - 2)
+            for j in lanes:
+                if k < 7:
+                    reduce(c, j, k - 1).start()
+                else:
+                    gather(c, j, 5).start()
+        elif k <= 12:
+            for j in lanes:
+                gather(c, j, 13 - k).wait()
+                gather(c, j, 12 - k).start()
+                if k == 12:
+                    give(c, j, False).start()
+        elif k == 13:
+            for j in lanes:
+                gather(c, j, 0).wait()
+                give(c, j, True).start()
+        else:
+            for j in lanes:
+                give(c, j, False).wait()
+                give(c, j, True).wait()
+
+    stages = 14
+    pl.semaphore_wait(barrier, len(peers))
+
+    def tick(t, carry):
+        for k in range(stages, 0, -1):
+
+            @pl.when((t >= GAP * k) & (t < chunks + GAP * k))
+            def _(k=k):
+                stage(k, t - GAP * k, range(PER_CHUNK))
+
+            @pl.when(t == GAP * k)
+            def _(k=k):
+                stage(k, 0, range(PER_CHUNK, PER_CHUNK + EXTRA))
+
+        @pl.when(t == 0)
+        def _():
+            for copy in side_copies:
+                copy.wait()
+            swap(0, False).start()
+            swap(0, True).start()
+
+        @pl.when((t >= 1) & (t < chunks))
+        def _():
+            load_block(t).wait()
+
+            @pl.when(t + 1 < chunks)
+            def _():
+                load_block(t + 1).start()
+
+            slot = lax.rem(t, 2)
+            for h in range(2):
+                g = jnp.dot(
+                    hid_t_ref[...], d_buf[slot, :, h * BLOCK // 2 : (h + 1) * BLOCK // 2], preferred_element_type=F32
+                )
+                tiles = jnp.concatenate([g[:, k * LANES : (k + 1) * LANES] for k in range(4)], axis=0)
+                held[h, pl.ds(t * PER_CHUNK, PER_CHUNK)] = tiles.reshape(PER_CHUNK, UNIT, LANES)
+            swap(t, False).start()
+
+        return carry
+
+    lax.fori_loop(0, chunks + GAP * stages, tick, 0)
+
+    block, lines = 1024, 64
+    total = jnp.zeros((lines, LANES), F32)
+    for h in range(2):
+
+        def add_squares(u, total, h=h):
+            here = full[h, u].reshape(UNIT // lines, lines, LANES)
+            return total + jnp.sum(here * here, axis=0)
+
+        total = lax.fori_loop(0, extra_at + 1, add_squares, total)
+        left = width - UNIT if h else EXTRA * UNIT - UNIT
+        here = full[h, extra_at + 1, 0:left, :].reshape(left // lines, lines, LANES)
+        total = total + jnp.sum(here * here, axis=0)
+    squares_ref[...] = jnp.sum(total.reshape(lines // 8, 8, LANES), axis=0)
+
+
+def exchange(side, dlog, hid_t):
+    width, rows_all = hid_t.shape
+    vocab = dlog.shape[1]
+    chunks, main, half = layout(width, vocab)
+    units = half // UNIT
+    vmem = pl.BlockSpec(memory_space=pltpu.VMEM)
+    anywhere = pl.BlockSpec(memory_space=pl.ANY)
+    shape = jax.ShapeDtypeStruct
+    full, squares = pl.pallas_call(
+        functools.partial(exchange_kernel, chunks),
+        out_shape=(shape((2, units, UNIT, LANES), F32), shape((8, LANES), F32)),
+        in_specs=[anywhere, anywhere, vmem],
+        out_specs=(vmem, vmem),
+        scratch_shapes=[
+            pltpu.VMEM((2, units, UNIT, LANES), F32),
+            pltpu.VMEM((units, UNIT, LANES), F32),
+            pltpu.VMEM((units, UNIT, LANES), F32),
+            pltpu.VMEM((2, rows_all, BLOCK), BF16),
+            pltpu.SemaphoreType.DMA((2, 2)),
+            pltpu.SemaphoreType.DMA((2,)),
+            pltpu.SemaphoreType.DMA((chunks + 1, 2)),
+            pltpu.SemaphoreType.DMA((chunks, PER_CHUNK, 14, 2)),
+            pltpu.SemaphoreType.DMA((EXTRA, 14, 2)),
+        ],
+        compiler_params=pltpu.CompilerParams(collective_id=0, has_side_effects=True, vmem_limit_bytes=63_000_000),
+        name="exchange",
+    )(side.reshape(2, side.shape[1] // UNIT, UNIT, LANES), dlog, hid_t)
+    return full.reshape(2 * half, LANES), squares
+
+
+def finish_kernel(main, half, count, full, squares_ref, out_ref, enc_ref, pred_ref, bias_ref, joint_ref, loss_ref, buf, side_buf, sems):
+    width, vocab = out_ref.shape
+    squares = jnp.sum(jnp.sum(squares_ref[...], axis=0, keepdims=True), axis=1, keepdims=True)
+    scale = lax.rsqrt(squares * (1.0 / count) + EPS)
+    copies = []
+    steps = vocab // CHUNK
+    per = CHUNK // LANES
+    for c in range(steps):
+        slot = c % buf.shape[0]
+        if c >= buf.shape[0]:
+            copies[c - buf.shape[0]].wait()
+        for k in range(per):
+            v = c * per + k
+            row = v % 8 // 4 * half + (v // 8 + 1) * main + v % 4 * width
+            buf[slot, :, k * LANES : (k + 1) * LANES] = full[row : row + width, :] * scale
+        copy = pltpu.make_async_copy(buf.at[slot], out_ref.at[:, pl.ds(c * CHUNK, CHUNK)], sems.at[slot])
+        copy.start()
+        copies.append(copy)
+    extra = half - EXTRA * UNIT
+    side_copies = []
+    for i, ref in enumerate((enc_ref, pred_ref)):
+        for k in range(width // LANES):
+            row = i * half + (k * width if k < 4 else extra)
+            side_buf[i, :, k * LANES : (k + 1) * LANES] = full[row : row + width, :] * scale
+        copy = pltpu.make_async_copy(side_buf.at[i], ref, sems.at[buf.shape[0] + i])
+        copy.start()
+        side_copies.append(copy)
+    row = extra + width
+    for k in range(vocab // LANES):
+        bias_ref[:, k * LANES : (k + 1) * LANES] = full[row + k : row + k + 1, :] * scale
+    row += vocab // LANES
+    for k in range(width // LANES):
+        joint_ref[:, k * LANES : (k + 1) * LANES] = full[row + k : row + k + 1, :] * scale
+    row = half + extra + width
+    loss = jnp.sum(full[row : row + 1, :], axis=1, keepdims=True)
+    labels = jnp.sum(full[row + 1 : row + 2, :], axis=1, keepdims=True)
+    loss_ref[...] = jnp.broadcast_to(loss / labels, loss_ref.shape)
+    for copy in copies[-buf.shape[0] :] + side_copies:
+        copy.wait()
+
+
+def finish(full, squares, width, vocab, count):
+    _, main, half = layout(width, vocab)
+    vmem = pl.BlockSpec(memory_space=pltpu.VMEM)
+    anywhere = pl.BlockSpec(memory_space=pl.ANY)
+    shape = jax.ShapeDtypeStruct
+    return pl.pallas_call(
+        functools.partial(finish_kernel, main, half, float(count)),
+        out_shape=(
+            shape((width, vocab), F32), shape((width, width), F32), shape((width, width), F32),
+            shape((1, vocab), F32), shape((1, width), F32), shape((1, LANES), F32),
+        ),
+        in_specs=[vmem, vmem],
+        out_specs=(anywhere, anywhere, anywhere, vmem, vmem, vmem),
+        scratch_shapes=[
+            pltpu.VMEM((4, width, CHUNK), F32),
+            pltpu.VMEM((2, width, width), F32),
+            pltpu.SemaphoreType.DMA((6,)),
+        ],
+        compiler_params=pltpu.CompilerParams(vmem_limit_bytes=40_000_000),
+        name="finish",
+    )(full, squares)
+
+
 def per_device(enc, pred, labels, frame_len, label_len, w_enc, w_pred, b_joint, w_out, b_out):
     width, vocab = w_out.shape
-    g_out, g_side = local_grads(enc, pred, labels, frame_len, label_len, w_enc, w_pred, b_joint, w_out, b_out)
-    g_out, g_side = lax.psum((g_out, g_side), AXES)
-    at = 2 * width
-    bias_rows = -(-vocab // width)
-    grads = g_side[: at + 1 + bias_rows, :]
-    squares = jnp.sum(g_out * g_out) + jnp.sum(grads * grads)
+    sums = local_grads(enc, pred, labels, frame_len, label_len, w_enc, w_pred, b_joint, w_out, b_out)
+    full, squares = exchange(*sums)
     count = w_enc.size + w_pred.size + w_out.size + b_out.size + b_joint.size
-    scale = lax.rsqrt(squares / jnp.float32(count) + EPS)
-    g_side_scaled = grads * scale
-    bias_out = g_side_scaled[at + 1 :, :].reshape(-1)[:vocab]
-    loss_sum, label_sum = jnp.sum(g_side[at + 1 + bias_rows : at + 3 + bias_rows, :LANES], axis=1)
-    return (
-        g_side_scaled[:width],
-        g_side_scaled[width:at],
-        g_out * scale,
-        bias_out,
-        g_side_scaled[at],
-        loss_sum / label_sum,
-    )
+    out, g_enc, g_pred, bias, joint, loss = finish(full, squares, width, vocab, count)
+    return g_enc, g_pred, out, bias.reshape(vocab), joint.reshape(width), loss[0, 0]
 
 
 def solution(mesh):

time: 280 us -> 162 us (0.58)
  waiting for transfers between devices: 175 us -> 0 us
  Pallas kernels: 57.1 us -> 150 us
  other arithmetic: 21.5 us -> 0.61 us
  between operations: 17.9 us -> 0.67 us
    psum x1 -> x0, waiting for transfers between devices: 175 us -> none  [per_device(): g_out, g_side = lax.psum((g_out, g_side), AXES)]
    pallas_call x1 -> x3, Pallas kernels: 57.1 us -> 150 us  [the longest x1 97.3 us: exchange(): pl.pallas_call(functools.partial(exchange_kernel, chunks), out_shape=(sha...]
    reduce_sum x3 -> x0, other arithmetic: 11.4 us -> none  [the longest x2 10.7 us: per_device(): squares = jnp.sum(g_out * g_out) + jnp.sum(grads * grads)]
    mul x2 -> x0, other arithmetic: 10 us -> none  [the longest x1 9.83 us: per_device(): g_out * scale]
    unnamed x3 -> x5, local copies, waits for them, and re-layouts: 1.42 us -> 7.11 us
    slice x4 -> x0, local copies, waits for them, and re-layouts: 3.13 us -> none  [the longest x1 1.91 us: per_device(): g_side_scaled[width:at]]
  transfers between devices with their start and end apart: 1 -> 0, of which waited for: 1 -> 0; matrix products, arithmetic and copies ran while one was open for 0% -> 0% of each run, Pallas kernels for 0% -> 0%
where the time goes in v3:
time: 162 us; the launch traced here: 161 us
  Pallas kernels  150 us (93%)
  local copies, waits for them, and re-layouts  9.68 us (6%)
    pallas_call x1, Pallas kernels, exchange(): pl.pallas_call(functools.partial(exchange_kernel, chunks), out_shape=(sha...  97.3 us
    pallas_call x1, Pallas kernels, local_grads(): pl.pallas_call(local_kernel, out_shape=(shape((2, side_rows, LANES), F32)...  47.2 us
    unnamed x5, local copies, waits for them, and re-layouts  7.11 us
    pallas_call x1, Pallas kernels, finish(): pl.pallas_call(functools.partial(finish_kernel, main, half, float(count))...  5.88 us

profile of v3, /device:TPU:1, one launch (start us, length us, event | category | flops | bytes accessed | tf_op | source)
XLA Modules:
  0.0 161.3 jit_solution(2606654474455223583)
XLA Ops:
  0.6 1.3 reshape.30.b_joint_ref
  1.9 1.3 reshape.31.b_out_ref
  3.2 1.4 copy.16.pred_ref
  4.6 47.2 %local_grads.1 = (f32[2,3584,128]{2,1,0:T(8,128)}, bf16[1664,4096]{1,0:T(8,128)(2,1)}, bf16[640,1664]{1,0:T(8,128)(2,1)}) custom-call(s32[2,16]{1,0:T(2,128)} %labels_ref.1, s32[2]{0:T(128)} %frame_ref.1, s32[2]{0:T(128)} %label_ref.1, bf16[2,48,640]{2,1,0:T(8,128)(2,1)} %enc_ref.1, bf16[2,17,640]{2,1,0:T(8,128)(2,1)} %copy.16.pred_ref, ...), custom_call_target="tpu_custom_call" | custom-call | tf_op jit(solution)/shard_map/local_grads/pallas_call | solution.py:280
  51.8 97.3 %exchange.1 = (f32[2,27,512,128]{3,2,1,0:T(8,128)}, f32[8,128]{1,0:T(8,128)}) custom-call(f32[2,7,512,128]{3,2,1,0:T(8,128)} %bitcast.6, bf16[1664,4096]{1,0:T(8,128)(2,1)} %get-tuple-element.18.dlog_ref, bf16[640,1664]{1,0:T(8,128)(2,1)} %get-tuple-element.19.hid_t_ref), custom_call_target="tpu_custom_call" | custom-call | tf_op jit(solution)/shard_map/exchange/pallas_call | solution.py:515
  149.1 0.0 copy-start
  149.1 5.0 %copy-done = f32[2,27,512,128]{3,2,1,0:T(8,128)S(1)} copy-done((f32[2,27,512,128]{3,2,1,0:T(8,128)S(1)}, f32[2,27,512,128]{3,2,1,0:T(8,128)}, u32[]{:S(2)}) %copy-start) | copy-done | bytes 14155800
  154.1 0.0 copy-start.1
  154.1 0.7 copy-done.1
  154.8 5.9 %finish.1 = (f32[640,4096]{1,0:T(8,128)}, f32[640,640]{1,0:T(8,128)}, f32[640,640]{1,0:T(8,128)}, f32[1,4096]{1,0:T(1,128)}, f32[1,640]{1,0:T(1,128)S(1)}, /*index=5*/f32[1,128]{1,0:T(1,128)}) custom-call(f32[27648,128]{1,0:T(8,128)S(1)} %bitcast.5, f32[8,128]{1,0:T(8,128)S(1)} %copy-done.1), custom_call_target="tpu_custom_call" | custom-call | tf_op jit(solution)/shard_map/finish/pallas_call | solution.py:583
  160.7 0.6 reduce
Async XLA Ops:
  149.1 5.0 %copy-start = (f32[2,27,512,128]{3,2,1,0:T(8,128)S(1)}, f32[2,27,512,128]{3,2,1,0:T(8,128)}, u32[]{:S(2)}) copy-start(f32[2,27,512,128]{3,2,1,0:T(8,128)} %get-tuple-element.20) | copy-start | bytes 42467332
  154.1 0.7 copy-start.1

commit v4 on v3

--- a/solution.py
+++ b/solution.py
@@ -250,6 +250,7 @@
 PER_CHUNK = 5
 BLOCK = 1024
 GAP = 2
+GROUPS = ((0,), (1,), (2, 3), (4, 5))
 EXTRA = 2
 
 
@@ -310,8 +311,8 @@
 
 
 def exchange_kernel(
-    chunks, side_ref, dlog_ref, hid_t_ref, full, squares_ref, held, from_core, arrived, d_buf,
-    side_sems, d_sems, core_sems, step_sems, extra_sems,
+    chunks, side_ref, dlog_ref, hid_t_ref, full_ref, squares_ref, full, held, from_core, arrived, d_buf, total_ref,
+    out_sems, side_sems, d_sems, core_sems, step_sems, extra_sems,
 ):
     dp, x = lax.axis_index("dp"), lax.axis_index("rep")
     core = lax.rem(dp, 2)
@@ -330,12 +331,29 @@
         second = lax.rem((turn + s) // 3 + core, 2)
         peer = second * (3 - v) + (1 - second) * (v + 1 - 2 * lax.rem(v, 2))
         bit = second * (v // 2) + (1 - second) * lax.rem((v + 1) // 2, 2)
-        where = list(place)
-        where[axis] = peer
-        return device(*where, core), bit
-
+        return axis, peer, bit
+
+    def peers_of(turn, group):
+        found = []
+        for mask in range(1, 1 << len(group)):
+            flips = [i for i in range(len(group)) if mask >> i & 1]
+            where = list(place)
+            for i in flips:
+                axis, peer, _ = link(turn, group[i])
+                where[axis] = peer
+            found.append((flips, device(*where, core)))
+        return found
+
+    turns = list(range(PER_CHUNK)) + [5, 2]
+    bits = [[link(turn, s)[2] for s in range(6)] for turn in turns]
     barrier = pltpu.get_barrier_semaphore()
-    peers = [other_core] + [link(p, 0)[0] for p in range(6)]
+    greeted = {}
+    for turn in range(6):
+        for group in GROUPS:
+            for flips, peer in peers_of(turn, group):
+                key = frozenset((turn + group[i]) % 6 for i in flips)
+                greeted[key] = peer
+    peers = [other_core] + list(greeted.values())
     for peer in peers:
         pl.semaphore_signal(barrier, inc=1, device_id=peer, device_id_type=pl.DeviceIdType.MESH)
 
@@ -355,12 +373,11 @@
 
     load_block(1).start()
 
-    turns = list(range(PER_CHUNK)) + [5, 2]
     offsets = []
-    for turn in turns:
+    for line_bits in bits:
         line = [0]
         for s in range(6):
-            line.append(line[-1] + link(turn, s)[1] * (UNIT >> (s + 1)))
+            line.append(line[-1] + line_bits[s] * (UNIT >> (s + 1)))
         offsets.append(line)
 
     def rows(start, n):
@@ -384,70 +401,126 @@
             held.at[1 - core, units], from_core.at[units], core_sems, (chunks if extra else c,), other_core
         )
 
-    def reduce(c, j, s):
-        peer, bit = link(turns[j], s)
-        n = UNIT >> (s + 1)
+    lands, numbers = [], []
+    at = number = 0
+    for group in GROUPS:
+        count = (1 << len(group)) - 1
+        lands.append(at)
+        numbers.append(number)
+        at += count * (UNIT >> (group[-1] + 1))
+        number += count
+    per_way = number
+
+    def reduce(c, j, g):
+        group = GROUPS[g]
+        n = UNIT >> (group[-1] + 1)
         u = unit_of(c, j)
-        return remote(
-            held.at[core, u, rows(offsets[j][s] + (1 - bit) * n, n)],
-            arrived.at[u, pl.ds(UNIT - 2 * n, n)],
-            *sem_of(c, j, s), peer,
-        )
-
-    def add_reduce(c, j, s):
-        n = UNIT >> (s + 1)
+        copies = []
+        for m, (flips, peer) in enumerate(peers_of(turns[j], group)):
+            start = offsets[j][group[0]]
+            for i, s in enumerate(group):
+                bit = bits[j][s]
+                start = start + (1 - bit if i in flips else bit) * (UNIT >> (s + 1))
+            copies.append(
+                remote(
+                    held.at[core, u, rows(start, n)], arrived.at[u, pl.ds(lands[g] + m * n, n)],
+                    *sem_of(c, j, numbers[g] + m), peer,
+                )
+            )
+        return copies
+
+    def add_reduce(c, j, g):
+        group = GROUPS[g]
+        n = UNIT >> (group[-1] + 1)
         u = unit_of(c, j)
-        here = rows(offsets[j][s + 1], n)
-        total = held[core, u, here, :] + arrived[u, pl.ds(UNIT - 2 * n, n), :]
-        if s < 5:
+        here = rows(offsets[j][group[-1] + 1], n)
+        total = held[core, u, here, :]
+        for m in range((1 << len(group)) - 1):
+            total = total + arrived[u, pl.ds(lands[g] + m * n, n), :]
+        if g < len(GROUPS) - 1:
             held[core, u, here, :] = total
         else:
             full[core, u, here, :] = total
 
-    def gather(c, j, s):
-        here = full.at[core, unit_of(c, j), rows(offsets[j][s + 1], UNIT >> (s + 1))]
-        return remote(here, here, *sem_of(c, j, 6 + s), link(turns[j], s)[0])
+    def gather(c, j, g):
+        group = GROUPS[g]
+        here = full.at[core, unit_of(c, j), rows(offsets[j][group[-1] + 1], UNIT >> (group[-1] + 1))]
+        return [
+            remote(here, here, *sem_of(c, j, per_way + numbers[g] + m), peer)
+            for m, (_, peer) in enumerate(peers_of(turns[j], group))
+        ]
 
     def give(c, j, late):
         n = UNIT // 2
-        bit = link(turns[j], 0)[1]
+        bit = bits[j][0]
         start = (1 - bit) * n if late else bit * n
         here = full.at[core, unit_of(c, j), rows(start, n)]
-        return remote(here, here, *sem_of(c, j, 13 if late else 12), other_core)
+        return [remote(here, here, *sem_of(c, j, 2 * per_way + late), other_core)]
+
+    def put(c, extra):
+        units = pl.ds(extra_at, EXTRA) if extra else pl.ds(c * PER_CHUNK, PER_CHUNK)
+        return [
+            pltpu.make_async_copy(full.at[h, units], full_ref.at[h, units], out_sems.at[chunks if extra else c, h])
+            for h in range(2)
+        ]
+
+    def start(copies):
+        for copy in copies:
+            copy.start()
+
+    def wait(copies):
+        for copy in copies:
+            copy.wait()
+
+    lines = 64
+
+    def add_squares(here):
+        here = here.reshape(here.shape[0] // lines, lines, LANES)
+        total_ref[...] = total_ref[...] + jnp.sum(here * here, axis=0)
+
+    last = len(GROUPS) - 1
 
     def stage(k, c, lanes):
+        extra = lanes[0] >= PER_CHUNK
         if k == 1:
-            for extra in {j >= PER_CHUNK for j in lanes}:
-                swap(c, extra).wait()
-                units = pl.ds(extra_at, EXTRA) if extra else pl.ds(c * PER_CHUNK, PER_CHUNK)
-                held[core, units] = held[core, units] + from_core[units]
+            swap(c, extra).wait()
+            units = pl.ds(extra_at, EXTRA) if extra else pl.ds(c * PER_CHUNK, PER_CHUNK)
+            held[core, units] = held[core, units] + from_core[units]
             for j in lanes:
-                reduce(c, j, 0).start()
-        elif k <= 7:
+                start(reduce(c, j, 0))
+        elif k <= last + 2:
             for j in lanes:
-                reduce(c, j, k - 2).wait()
+                wait(reduce(c, j, k - 2))
                 add_reduce(c, j, k - 2)
             for j in lanes:
-                if k < 7:
-                    reduce(c, j, k - 1).start()
-                else:
-                    gather(c, j, 5).start()
-        elif k <= 12:
+                start(reduce(c, j, k - 1) if k <= last + 1 else gather(c, j, last))
+        elif k <= 2 * last + 2:
+            g = 2 * last + 2 - k
             for j in lanes:
-                gather(c, j, 13 - k).wait()
-                gather(c, j, 12 - k).start()
-                if k == 12:
-                    give(c, j, False).start()
-        elif k == 13:
+                wait(gather(c, j, g + 1))
+                start(gather(c, j, g))
+                if g == 0:
+                    start(give(c, j, 0))
+        elif k == 2 * last + 3:
             for j in lanes:
-                gather(c, j, 0).wait()
-                give(c, j, True).start()
+                wait(gather(c, j, 0))
+                start(give(c, j, 1))
         else:
             for j in lanes:
-                give(c, j, False).wait()
-                give(c, j, True).wait()
-
-    stages = 14
+                wait(give(c, j, 0))
+                wait(give(c, j, 1))
+            start(put(c, extra))
+            for h in range(2):
+                if extra:
+                    left = width - UNIT if h else EXTRA * UNIT - UNIT
+                    add_squares(full[h, extra_at])
+                    add_squares(full[h, extra_at + 1, 0:left, :])
+                else:
+                    for j in lanes:
+                        add_squares(full[h, unit_of(c, j)])
+
+    stages = 2 * last + 4
+    total_ref[...] = jnp.zeros_like(total_ref)
     pl.semaphore_wait(barrier, len(peers))
 
     def tick(t, carry):
@@ -489,19 +562,10 @@
 
     lax.fori_loop(0, chunks + GAP * stages, tick, 0)
 
-    block, lines = 1024, 64
-    total = jnp.zeros((lines, LANES), F32)
-    for h in range(2):
-
-        def add_squares(u, total, h=h):
-            here = full[h, u].reshape(UNIT // lines, lines, LANES)
-            return total + jnp.sum(here * here, axis=0)
-
-        total = lax.fori_loop(0, extra_at + 1, add_squares, total)
-        left = width - UNIT if h else EXTRA * UNIT - UNIT
-        here = full[h, extra_at + 1, 0:left, :].reshape(left // lines, lines, LANES)
-        total = total + jnp.sum(here * here, axis=0)
-    squares_ref[...] = jnp.sum(total.reshape(lines // 8, 8, LANES), axis=0)
+    squares_ref[...] = jnp.sum(total_ref[...].reshape(lines // 8, 8, LANES), axis=0)
+    for c in range(chunks):
+        wait(put(c, False))
+    wait(put(0, True))
 
 
 def exchange(side, dlog, hid_t):
@@ -509,6 +573,7 @@
     vocab = dlog.shape[1]
     chunks, main, half = layout(width, vocab)
     units = half // UNIT
+    messages = 2 * sum((1 << len(group)) - 1 for group in GROUPS) + 2
     vmem = pl.BlockSpec(memory_space=pltpu.VMEM)
     anywhere = pl.BlockSpec(memory_space=pl.ANY)
     shape = jax.ShapeDtypeStruct
@@ -516,17 +581,20 @@
         functools.partial(exchange_kernel, chunks),
         out_shape=(shape((2, units, UNIT, LANES), F32), shape((8, LANES), F32)),
         in_specs=[anywhere, anywhere, vmem],
-        out_specs=(vmem, vmem),
+        out_specs=(anywhere, vmem),
         scratch_shapes=[
+            pltpu.VMEM((2, units, UNIT, LANES), F32),
             pltpu.VMEM((2, units, UNIT, LANES), F32),
             pltpu.VMEM((units, UNIT, LANES), F32),
             pltpu.VMEM((units, UNIT, LANES), F32),
             pltpu.VMEM((2, rows_all, BLOCK), BF16),
+            pltpu.VMEM((64, LANES), F32),
+            pltpu.SemaphoreType.DMA((chunks + 1, 2)),
             pltpu.SemaphoreType.DMA((2, 2)),
             pltpu.SemaphoreType.DMA((2,)),
             pltpu.SemaphoreType.DMA((chunks + 1, 2)),
-            pltpu.SemaphoreType.DMA((chunks, PER_CHUNK, 14, 2)),
-            pltpu.SemaphoreType.DMA((EXTRA, 14, 2)),
+            pltpu.SemaphoreType.DMA((chunks, PER_CHUNK, messages, 2)),
+            pltpu.SemaphoreType.DMA((EXTRA, messages, 2)),
         ],
         compiler_params=pltpu.CompilerParams(collective_id=0, has_side_effects=True, vmem_limit_bytes=63_000_000),
         name="exchange",
@@ -534,8 +602,20 @@
     return full.reshape(2 * half, LANES), squares
 
 
-def finish_kernel(main, half, count, full, squares_ref, out_ref, enc_ref, pred_ref, bias_ref, joint_ref, loss_ref, buf, side_buf, sems):
+def finish_kernel(main, half, count, full_ref, squares_ref, out_ref, enc_ref, pred_ref, bias_ref, joint_ref, loss_ref, full, buf, side_buf, load_sems, sems):
     width, vocab = out_ref.shape
+    chunks = 1 + vocab // BLOCK
+    loads = []
+    for h in range(2):
+        spans = [(c * main, main) for c in range(chunks)] + [(chunks * main, half - chunks * main)]
+        for c, (at, n) in enumerate(spans):
+            here = pl.ds(h * half + at, n)
+            loads.append(pltpu.make_async_copy(full_ref.at[here, :], full.at[here, :], load_sems.at[h, c]))
+    arrivals = {}
+    for c in [*range(1, chunks), 0, chunks]:
+        arrivals[c] = [loads[c], loads[c + chunks + 1]]
+        for copy in arrivals[c]:
+            copy.start()
     squares = jnp.sum(jnp.sum(squares_ref[...], axis=0, keepdims=True), axis=1, keepdims=True)
     scale = lax.rsqrt(squares * (1.0 / count) + EPS)
     copies = []
@@ -545,6 +625,7 @@
         slot = c % buf.shape[0]
         if c >= buf.shape[0]:
             copies[c - buf.shape[0]].wait()
+        arrivals[c // 2 + 1][c % 2].wait()
         for k in range(per):
             v = c * per + k
             row = v % 8 // 4 * half + (v // 8 + 1) * main + v % 4 * width
@@ -552,6 +633,9 @@
         copy = pltpu.make_async_copy(buf.at[slot], out_ref.at[:, pl.ds(c * CHUNK, CHUNK)], sems.at[slot])
         copy.start()
         copies.append(copy)
+    for c in (0, chunks):
+        for copy in arrivals[c]:
+            copy.wait()
     extra = half - EXTRA * UNIT
     side_copies = []
     for i, ref in enumerate((enc_ref, pred_ref)):
@@ -586,14 +670,16 @@
             shape((width, vocab), F32), shape((width, width), F32), shape((width, width), F32),
             shape((1, vocab), F32), shape((1, width), F32), shape((1, LANES), F32),
         ),
-        in_specs=[vmem, vmem],
+        in_specs=[anywhere, vmem],
         out_specs=(anywhere, anywhere, anywhere, vmem, vmem, vmem),
         scratch_shapes=[
+            pltpu.VMEM(full.shape, F32),
             pltpu.VMEM((4, width, CHUNK), F32),
             pltpu.VMEM((2, width, width), F32),
+            pltpu.SemaphoreType.DMA((2, 2 + vocab // BLOCK)),
             pltpu.SemaphoreType.DMA((6,)),
         ],
-        compiler_params=pltpu.CompilerParams(vmem_limit_bytes=40_000_000),
+        compiler_params=pltpu.CompilerParams(vmem_limit_bytes=63_000_000),
         name="finish",
     )(full, squares)
 

time: 162 us -> 156 us (0.963)
  local copies, waits for them, and re-layouts: 9.68 us -> 3.99 us
    pallas_call x1, Pallas kernels: 97.3 us -> 90.3 us  [exchange(): pl.pallas_call(functools.partial(exchange_kernel, chunks), out_shape=(sha...]
    pallas_call x1, Pallas kernels: 5.88 us -> 12 us  [finish(): pl.pallas_call(functools.partial(finish_kernel, main, half, float(count))...]
    unnamed x5 -> x1, local copies, waits for them, and re-layouts: 7.11 us -> 1.42 us
where the time goes in v4:
time: 156 us; the launch traced here: 155 us
  Pallas kernels  150 us (96%)
  local copies, waits for them, and re-layouts  3.99 us (3%)
    pallas_call x1, Pallas kernels, exchange(): pl.pallas_call(functools.partial(exchange_kernel, chunks), out_shape=(sha...  90.3 us
    pallas_call x1, Pallas kernels, local_grads(): pl.pallas_call(local_kernel, out_shape=(shape((2, side_rows, LANES), F32)...  47.2 us
    pallas_call x1, Pallas kernels, finish(): pl.pallas_call(functools.partial(finish_kernel, main, half, float(count))...  12 us

profile of v4, /device:TPU:1, one launch (start us, length us, event | category | flops | bytes accessed | tf_op | source)
XLA Modules:
  0.0 155.5 jit_solution(11596356299327538127)
XLA Ops:
  0.6 1.3 reshape.30.b_joint_ref
  1.9 1.3 reshape.31.b_out_ref
  3.2 1.4 copy.16.pred_ref
  4.6 47.2 %local_grads.1 = (f32[2,3584,128]{2,1,0:T(8,128)}, bf16[1664,4096]{1,0:T(8,128)(2,1)}, bf16[640,1664]{1,0:T(8,128)(2,1)}) custom-call(s32[2,16]{1,0:T(2,128)} %labels_ref.1, s32[2]{0:T(128)} %frame_ref.1, s32[2]{0:T(128)} %label_ref.1, bf16[2,48,640]{2,1,0:T(8,128)(2,1)} %enc_ref.1, bf16[2,17,640]{2,1,0:T(8,128)(2,1)} %copy.16.pred_ref, ...), custom_call_target="tpu_custom_call" | custom-call | tf_op jit(solution)/shard_map/local_grads/pallas_call | solution.py:281
  51.8 90.3 %exchange.1 = (f32[2,27,512,128]{3,2,1,0:T(8,128)}, f32[8,128]{1,0:T(8,128)}) custom-call(f32[2,7,512,128]{3,2,1,0:T(8,128)} %bitcast.6, bf16[1664,4096]{1,0:T(8,128)(2,1)} %get-tuple-element.18.dlog_ref, bf16[640,1664]{1,0:T(8,128)(2,1)} %get-tuple-element.19.hid_t_ref), custom_call_target="tpu_custom_call" | custom-call | tf_op jit(solution)/shard_map/exchange/pallas_call | solution.py:580
  142.1 12.0 %finish.1 = (f32[640,4096]{1,0:T(8,128)}, f32[640,640]{1,0:T(8,128)}, f32[640,640]{1,0:T(8,128)}, f32[1,4096]{1,0:T(1,128)}, f32[1,640]{1,0:T(1,128)}, /*index=5*/f32[1,128]{1,0:T(1,128)}) custom-call(f32[27648,128]{1,0:T(8,128)} %bitcast.5, f32[8,128]{1,0:T(8,128)} %get-tuple-element.21.squares_ref), custom_call_target="tpu_custom_call" | custom-call | tf_op jit(solution)/shard_map/finish/pallas_call | solution.py:667
  154.2 1.3 reduce

commit v5 on v4

--- a/solution.py
+++ b/solution.py
@@ -22,9 +22,11 @@
     labels_ref, frame_ref, label_ref, enc_ref, pred_ref, w_enc_ref, w_pred_ref, b_joint_ref, w_out_hbm, b_out_ref,
     side_ref, dlog_ref, hid_t_ref,
     hid, hid_t, logits, dhid, dlog, top, tot, lse, occ, emit_occ, blank_occ, target, blank_d, emit_d, alpha_d,
-    beta_d, below_d, right_d, pred_pad, dpred_pad, denc, bias_acc, slabs, tail, w_out_ref, sems, side_sems, load_sem, hid_sem,
+    beta_d, below_d, right_d, pred_pad, dpred_pad, denc, bias_acc, slabs, tail, w_out_ref, b_joint_row, b_out_row, sems, side_sems, load_sem, hid_sem,
 ):
     utts, frames, _ = enc_ref.shape
+    b_joint_row[...] = b_joint_ref[...].astype(F32).reshape(b_joint_row.shape)
+    b_out_row[...] = b_out_ref[...].astype(F32).reshape(b_out_row.shape)
     slots = pred_ref.shape[1]
     width = w_enc_ref.shape[1]
     vocab = w_out_ref.shape[1]
@@ -45,7 +47,7 @@
     enc_proj = [jnp.dot(enc_ref[i], w_enc_ref[...], preferred_element_type=F32) for i in range(utts)]
     for i in range(utts):
         pred_pad[SLOT * i : SLOT * i + slots, :] = pred_ref[i]
-    pred_proj = jnp.dot(pred_pad[...], w_pred_ref[...], preferred_element_type=F32) + b_joint_ref[...].astype(F32)
+    pred_proj = jnp.dot(pred_pad[...], w_pred_ref[...], preferred_element_type=F32) + b_joint_row[...]
     for i, u, row, col in blocks:
         hid[row : row + frames, :] = jnp.tanh(enc_proj[i] + pred_proj[col : col + 1, :]).astype(BF16)
     hid_t[...] = hid[...].T
@@ -60,11 +62,11 @@
     picks = picks.astype(F32).astype(BF16)
     w_pick = jnp.dot(w_out_ref[...], picks, preferred_element_type=F32).astype(BF16)
     b_pick = jnp.dot(
-        jnp.broadcast_to(b_out_ref[...], (16, vocab)), picks, preferred_element_type=F32
+        jnp.broadcast_to(b_out_row[...], (16, vocab)).astype(BF16), picks, preferred_element_type=F32
     )[:1, :]
     w_blank = jnp.broadcast_to(w_out_ref[:, :1].astype(F32), (width, LANES)).astype(BF16)
     w_two = jnp.concatenate([w_pick, w_blank], axis=1)
-    b_blank = b_out_ref[:, :1].astype(F32)
+    b_blank = b_out_row[:, :1]
 
     top[...] = jnp.full_like(top, NEG)
     tot[...] = jnp.zeros_like(tot)
@@ -72,7 +74,7 @@
     def forward(c, carry):
         cols = pl.ds(pl.multiple_of(c * CHUNK, CHUNK), CHUNK)
         w_c = w_out_ref[:, cols]
-        b_c = b_out_ref[:, cols].astype(F32)
+        b_c = b_out_row[:, cols]
         for r in range(0, rows_all, ROWS):
             z = jnp.dot(hid[r : r + ROWS, :], w_c, preferred_element_type=F32) + b_c
             logits[r : r + ROWS, cols] = z
@@ -300,6 +302,8 @@
             pltpu.VMEM((2, width // LANES, width, LANES), F32),
             pltpu.VMEM((2, side_rows - width // LANES * width, LANES), F32),
             pltpu.VMEM((width, vocab), BF16),
+            pltpu.VMEM((1, width), F32),
+            pltpu.VMEM((1, vocab), F32),
             pltpu.SemaphoreType.DMA((2,)),
             pltpu.SemaphoreType.DMA((2, width // LANES + 1)),
             pltpu.SemaphoreType.DMA(()),
@@ -307,7 +311,7 @@
         ],
         compiler_params=pltpu.CompilerParams(vmem_limit_bytes=66_000_000),
         name="local_grads",
-    )(labels, frame_len, label_len, enc, pred, w_enc, w_pred, b_joint.reshape(1, width), w_out, b_out.reshape(1, vocab))
+    )(labels, frame_len, label_len, enc, pred, w_enc, w_pred, b_joint, w_out, b_out)
 
 
 def exchange_kernel(
@@ -524,7 +528,7 @@
     pl.semaphore_wait(barrier, len(peers))
 
     def tick(t, carry):
-        for k in range(stages, 0, -1):
+        for k in range(1, stages + 1):
 
             @pl.when((t >= GAP * k) & (t < chunks + GAP * k))
             def _(k=k):
@@ -602,20 +606,8 @@
     return full.reshape(2 * half, LANES), squares
 
 
-def finish_kernel(main, half, count, full_ref, squares_ref, out_ref, enc_ref, pred_ref, bias_ref, joint_ref, loss_ref, full, buf, side_buf, load_sems, sems):
+def finish_kernel(main, half, count, full, squares_ref, out_ref, enc_ref, pred_ref, bias_ref, joint_ref, loss_ref, buf, side_buf, sems):
     width, vocab = out_ref.shape
-    chunks = 1 + vocab // BLOCK
-    loads = []
-    for h in range(2):
-        spans = [(c * main, main) for c in range(chunks)] + [(chunks * main, half - chunks * main)]
-        for c, (at, n) in enumerate(spans):
-            here = pl.ds(h * half + at, n)
-            loads.append(pltpu.make_async_copy(full_ref.at[here, :], full.at[here, :], load_sems.at[h, c]))
-    arrivals = {}
-    for c in [*range(1, chunks), 0, chunks]:
-        arrivals[c] = [loads[c], loads[c + chunks + 1]]
-        for copy in arrivals[c]:
-            copy.start()
     squares = jnp.sum(jnp.sum(squares_ref[...], axis=0, keepdims=True), axis=1, keepdims=True)
     scale = lax.rsqrt(squares * (1.0 / count) + EPS)
     copies = []
@@ -625,7 +617,6 @@
         slot = c % buf.shape[0]
         if c >= buf.shape[0]:
             copies[c - buf.shape[0]].wait()
-        arrivals[c // 2 + 1][c % 2].wait()
         for k in range(per):
             v = c * per + k
             row = v % 8 // 4 * half + (v // 8 + 1) * main + v % 4 * width
@@ -633,9 +624,6 @@
         copy = pltpu.make_async_copy(buf.at[slot], out_ref.at[:, pl.ds(c * CHUNK, CHUNK)], sems.at[slot])
         copy.start()
         copies.append(copy)
-    for c in (0, chunks):
-        for copy in arrivals[c]:
-            copy.wait()
     extra = half - EXTRA * UNIT
     side_copies = []
     for i, ref in enumerate((enc_ref, pred_ref)):
@@ -654,7 +642,7 @@
     row = half + extra + width
     loss = jnp.sum(full[row : row + 1, :], axis=1, keepdims=True)
     labels = jnp.sum(full[row + 1 : row + 2, :], axis=1, keepdims=True)
-    loss_ref[...] = jnp.broadcast_to(loss / labels, loss_ref.shape)
+    loss_ref[0, 0] = jnp.sum(loss / labels)
     for copy in copies[-buf.shape[0] :] + side_copies:
         copy.wait()
 
@@ -668,18 +656,16 @@
         functools.partial(finish_kernel, main, half, float(count)),
         out_shape=(
             shape((width, vocab), F32), shape((width, width), F32), shape((width, width), F32),
-            shape((1, vocab), F32), shape((1, width), F32), shape((1, LANES), F32),
+            shape((1, vocab), F32), shape((1, width), F32), shape((1, 1), F32),
         ),
-        in_specs=[anywhere, vmem],
-        out_specs=(anywhere, anywhere, anywhere, vmem, vmem, vmem),
+        in_specs=[vmem, vmem],
+        out_specs=(anywhere, anywhere, anywhere, vmem, vmem, pl.BlockSpec(memory_space=pltpu.SMEM)),
         scratch_shapes=[
-            pltpu.VMEM(full.shape, F32),
             pltpu.VMEM((4, width, CHUNK), F32),
             pltpu.VMEM((2, width, width), F32),
-            pltpu.SemaphoreType.DMA((2, 2 + vocab // BLOCK)),
             pltpu.SemaphoreType.DMA((6,)),
         ],
-        compiler_params=pltpu.CompilerParams(vmem_limit_bytes=63_000_000),
+        compiler_params=pltpu.CompilerParams(vmem_limit_bytes=40_000_000),
         name="finish",
     )(full, squares)
 
@@ -690,7 +676,7 @@
     full, squares = exchange(*sums)
     count = w_enc.size + w_pred.size + w_out.size + b_out.size + b_joint.size
     out, g_enc, g_pred, bias, joint, loss = finish(full, squares, width, vocab, count)
-    return g_enc, g_pred, out, bias.reshape(vocab), joint.reshape(width), loss[0, 0]
+    return g_enc, g_pred, out, bias.reshape(vocab), joint.reshape(width), loss.reshape(())
 
 
 def solution(mesh):

time: 156 us -> 152 us (0.974)
  Pallas kernels: 150 us -> 143 us
  local copies, waits for them, and re-layouts: 3.99 us -> 7.11 us
    pallas_call x1, Pallas kernels: 12 us -> 5.89 us  [finish(): pl.pallas_call(functools.partial(finish_kernel, main, half, float(count))...]
    unnamed x1 -> x5, local copies, waits for them, and re-layouts: 1.42 us -> 7.11 us
    reshape x2 -> x0, local copies, waits for them, and re-layouts: 2.57 us -> none  [the longest x1 1.31 us: local_grads(): b_out.reshape(1, vocab)]
where the time goes in v5:
time: 152 us
  Pallas kernels  143 us (94%)
  local copies, waits for them, and re-layouts  7.11 us (5%)
    pallas_call x1, Pallas kernels, exchange(): pl.pallas_call(functools.partial(exchange_kernel, chunks), out_shape=(sha...  89.8 us
    pallas_call x1, Pallas kernels, local_grads(): pl.pallas_call(local_kernel, out_shape=(shape((2, side_rows, LANES), F32)...  47.4 us
    unnamed x5, local copies, waits for them, and re-layouts  7.11 us
    pallas_call x1, Pallas kernels, finish(): pl.pallas_call(functools.partial(finish_kernel, main, half, float(count))...  5.89 us

profile of v5, /device:TPU:1, one launch (start us, length us, event | category | flops | bytes accessed | tf_op | source)
XLA Modules:
  0.0 151.5 jit_solution(15475856662507390702)
XLA Ops:
  0.6 1.4 copy.16.pred_ref
  2.0 47.4 %local_grads.1 = (f32[2,3584,128]{2,1,0:T(8,128)}, bf16[1664,4096]{1,0:T(8,128)(2,1)}, bf16[640,1664]{1,0:T(8,128)(2,1)}) custom-call(s32[2,16]{1,0:T(2,128)} %labels_ref.1, s32[2]{0:T(128)} %frame_ref.1, s32[2]{0:T(128)} %label_ref.1, bf16[2,48,640]{2,1,0:T(8,128)(2,1)} %enc_ref.1, bf16[2,17,640]{2,1,0:T(8,128)(2,1)} %copy.16.pred_ref, ...), custom_call_target="tpu_custom_call" | custom-call | tf_op jit(solution)/shard_map/local_grads/pallas_call | solution.py:283
  49.5 89.8 %exchange.1 = (f32[2,27,512,128]{3,2,1,0:T(8,128)}, f32[8,128]{1,0:T(8,128)}) custom-call(f32[2,7,512,128]{3,2,1,0:T(8,128)} %bitcast.5, bf16[1664,4096]{1,0:T(8,128)(2,1)} %get-tuple-element.18.dlog_ref, bf16[640,1664]{1,0:T(8,128)(2,1)} %get-tuple-element.19.hid_t_ref), custom_call_target="tpu_custom_call" | custom-call | tf_op jit(solution)/shard_map/exchange/pallas_call | solution.py:584
  139.3 0.0 copy-start
  139.3 5.0 %copy-done = f32[2,27,512,128]{3,2,1,0:T(8,128)S(1)} copy-done((f32[2,27,512,128]{3,2,1,0:T(8,128)S(1)}, f32[2,27,512,128]{3,2,1,0:T(8,128)}, u32[]{:S(2)}) %copy-start) | copy-done | bytes 14155800
  144.3 0.0 copy-start.1
  144.4 0.7 copy-done.1
  145.0 5.9 %finish.1 = (f32[640,4096]{1,0:T(8,128)}, f32[640,640]{1,0:T(8,128)}, f32[640,640]{1,0:T(8,128)}, f32[1,4096]{1,0:T(1,128)}, f32[1,640]{1,0:T(1,128)S(1)}, /*index=5*/f32[1,1]{1,0:T(1,128)}) custom-call(f32[27648,128]{1,0:T(8,128)S(1)} %bitcast.4, f32[8,128]{1,0:T(8,128)S(1)} %copy-done.1), custom_call_target="tpu_custom_call" | custom-call | tf_op jit(solution)/shard_map/finish/pallas_call | solution.py:655
  150.9 0.6 reduce
Async XLA Ops:
  139.3 5.0 %copy-start = (f32[2,27,512,128]{3,2,1,0:T(8,128)S(1)}, f32[2,27,512,128]{3,2,1,0:T(8,128)}, u32[]{:S(2)}) copy-start(f32[2,27,512,128]{3,2,1,0:T(8,128)} %get-tuple-element.20) | copy-start | bytes 42467332
  144.3 0.7 copy-start.1
